TPU v7x, 32 devices: a whole 2x2x4 slice. The times are simulated.
32 devices in a mesh: gx: 4 (over y, core), gy: 2 (over x), gz: 4 (over z).
Axes of the slice: x: 2, y: 2, z: 4, core: 2. Of those that a mesh axis runs over, the one named last changes fastest.
Arguments:
- thermal_state: float32 [32, 16, 512], P('gx', 'gy', 'gz'), may hold values from 0.5 to 1.5
- diffusivity: float32 [32, 16, 512], P('gx', 'gy', 'gz'), may hold values from 1.1 to 13.2
- staggered_flux_density: float32 [3, 32, 16, 512], P(None, 'gx', 'gy', 'gz'), may hold values from -6 to 6
- bulk_motion: float32 [3, 32, 16, 512], P(None, 'gx', 'gy', 'gz'), may hold values from -3 to 3
- mass_per_volume: float32 [32, 16, 512], P('gx', 'gy', 'gz'), may hold values from 0.5 to 2
Outputs:
- temperature_out: float32 [32, 16, 512], P('gx', 'gy', 'gz')
- face_field_out: float32 [3, 32, 16, 512], P(None, 'gx', 'gy', 'gz')
All inputs are finite; a program needn't handle non-finite values.
Results may differ from a plain program's by a relative error of at most 0.00002.
Values sent between devices are 32-bit elements; how exact they have to be, the bound alone decides.
A program may use at most 128 MiB of HBM per device.

v0:
```python
import jax
import jax.numpy as jnp
from jax import lax
from jax.sharding import PartitionSpec as P

SECTIONS = 8


GAMMA = 5.0 / 3.0
FACE_FLOOR = 0.25
REFERENCE_SPOT = (0, 0, 0)


def extended(block, sides, width):
    for axis, dim in sides:
        count = lax.axis_size(axis)
        forward = [(i, i + 1) for i in range(count - 1)]
        forward.append((count - 1, 0))
        backward = [(target, source) for source, target in forward]
        low = lax.ppermute(
            lax.slice_in_dim(block, block.shape[dim] - width, None, axis=dim), axis, forward
        )
        high = lax.ppermute(lax.slice_in_dim(block, 0, width, axis=dim), axis, backward)
        block = jnp.concatenate([low, block, high], axis=dim)
    return block


def unit_step(direction, amount):
    return tuple((amount if candidate == direction else 0 for candidate in range(3)))


def combine_steps(left_step, right_step):
    return tuple(
        map(lambda first_part, second_part: first_part + second_part, left_step, right_step)
    )


def even_reach(amount):
    return (amount, amount, amount)


def sites_placed(source, ghost_layer_sites, offset, low_side, high_side):
    extents = source.shape[-3:]
    selector = [slice(None)] * (source.ndim - 3)
    for direction in range(3):
        interior = extents[direction] - 2 * ghost_layer_sites
        begin_at = ghost_layer_sites - low_side[direction] + offset[direction]
        selector.append(
            slice(begin_at, begin_at + interior + low_side[direction] + high_side[direction])
        )
    return source[tuple(selector)]


def trim_extent(source, ghost_layer_sites, amount):
    return sites_placed(
        source, ghost_layer_sites, REFERENCE_SPOT, even_reach(amount), even_reach(amount)
    )


def face_coefficients(diffusion_coefficient, interface_quantities, ghost_layer_sites, reach):
    interior_block = even_reach(reach)
    lookup_arrays = []
    for normal in range(3):
        backward = unit_step(normal, -1)
        kappa_face = 0.5 * (
            sites_placed(
                diffusion_coefficient,
                ghost_layer_sites,
                REFERENCE_SPOT,
                interior_block,
                interior_block,
            )
            + sites_placed(
                diffusion_coefficient, ghost_layer_sites, backward, interior_block, interior_block
            )
        )
        normal_part = sites_placed(
            interface_quantities[normal],
            ghost_layer_sites,
            REFERENCE_SPOT,
            interior_block,
            interior_block,
        )
        across = []
        for rotation in (1, 2):
            other_axis = (normal + rotation) % 3
            forward = unit_step(other_axis, 1)
            across.append(
                0.25
                * (
                    sites_placed(
                        interface_quantities[other_axis],
                        ghost_layer_sites,
                        REFERENCE_SPOT,
                        interior_block,
                        interior_block,
                    )
                    + sites_placed(
                        interface_quantities[other_axis],
                        ghost_layer_sites,
                        forward,
                        interior_block,
                        interior_block,
                    )
                    + sites_placed(
                        interface_quantities[other_axis],
                        ghost_layer_sites,
                        backward,
                        interior_block,
                        interior_block,
                    )
                    + sites_placed(
                        interface_quantities[other_axis],
                        ghost_layer_sites,
                        combine_steps(backward, forward),
                        interior_block,
                        interior_block,
                    )
                )
            )
        squared = normal_part * normal_part + across[0] * across[0] + across[1] * across[1]
        scaling = kappa_face / jnp.maximum(squared, FACE_FLOOR)
        lookup_arrays.append(
            (
                scaling * normal_part * normal_part,
                scaling * normal_part * across[0],
                scaling * normal_part * across[1],
            )
        )
    return lookup_arrays


def diffuse_thermal(profile, ghost_layer_sites, lookup_arrays, reach, target):
    interior_block = even_reach(target)
    balance = None
    for normal in range(3):
        upper_side = tuple((target + (1 if candidate == normal else 0) for candidate in range(3)))
        backward = unit_step(normal, -1)

        def shifted(offset):
            return sites_placed(profile, ghost_layer_sites, offset, interior_block, upper_side)

        slopes = []
        for rotation in (1, 2):
            other_axis = (normal + rotation) % 3
            forward = unit_step(other_axis, 1)
            rearward = unit_step(other_axis, -1)
            slopes.append(
                0.25
                * (
                    shifted(forward)
                    - shifted(rearward)
                    + shifted(combine_steps(backward, forward))
                    - shifted(combine_steps(backward, rearward))
                )
            )
        along_normal, along_first, along_second = [
            sites_placed(coefficient, reach, REFERENCE_SPOT, interior_block, upper_side)
            for coefficient in lookup_arrays[normal]
        ]
        face_flux = -(
            along_normal * (shifted(REFERENCE_SPOT) - shifted(backward))
            + along_first * slopes[0]
            + along_second * slopes[1]
        )
        length = face_flux.shape[normal]
        change = lax.slice_in_dim(face_flux, 1, length, axis=normal) - lax.slice_in_dim(
            face_flux, 0, length - 1, axis=normal
        )
        balance = -change if balance is None else balance - change
    return balance


def section_weights(total):
    first_rate = 4.0 / (total * total + total - 2)
    factors = [1.0 / 3.0, 1.0 / 3.0, 1.0 / 3.0]
    for ordinal in range(3, total + 1):
        factors.append((ordinal * ordinal + ordinal - 2) / (2.0 * ordinal * (ordinal + 1)))
    layout_recipe = [None, factors[1] * first_rate]
    for ordinal in range(2, total + 1):
        weight_prev = (2.0 * ordinal - 1.0) / ordinal * factors[ordinal] / factors[ordinal - 1]
        weight_older = -(ordinal - 1.0) / ordinal * factors[ordinal] / factors[ordinal - 2]
        rate_prev = weight_prev * first_rate
        rate_zero = -(1.0 - factors[ordinal - 1]) * rate_prev
        layout_recipe.append(
            (weight_prev, weight_older, 1.0 - weight_prev - weight_older, rate_prev, rate_zero)
        )
    return layout_recipe


def subdivision_advance(
    weights,
    interval_increment,
    newest_iterate,
    newest_extended,
    previous_iterate,
    previous_extended,
    initial,
    initial_margin,
    initial_derivative,
    zero_margin,
    lookup_arrays,
    reach,
):
    target = newest_extended - 1
    weight_prev, weight_older, weight_zero, rate_prev, rate_zero = weights
    prev_rate = diffuse_thermal(newest_iterate, newest_extended, lookup_arrays, reach, target)
    return (
        weight_prev * trim_extent(newest_iterate, newest_extended, target)
        + weight_older * trim_extent(previous_iterate, previous_extended, target)
        + weight_zero * trim_extent(initial, initial_margin, target)
        + rate_prev * interval_increment * prev_rate
        + rate_zero * interval_increment * trim_extent(initial_derivative, zero_margin, target)
    )


def fastest_characteristic(
    thermal_state, mass_per_volume, interface_quantities, bulk_motion, ghost_layer_sites
):
    interior_block = even_reach(1)
    centred = []
    for direction in range(3):
        centred.append(
            0.5
            * (
                sites_placed(
                    interface_quantities[direction],
                    ghost_layer_sites,
                    REFERENCE_SPOT,
                    interior_block,
                    interior_block,
                )
                + sites_placed(
                    interface_quantities[direction],
                    ghost_layer_sites,
                    unit_step(direction, 1),
                    interior_block,
                    interior_block,
                )
            )
        )
    moving = [
        sites_placed(
            bulk_motion[direction],
            ghost_layer_sites,
            REFERENCE_SPOT,
            interior_block,
            interior_block,
        )
        for direction in range(3)
    ]
    field_square = centred[0] * centred[0] + centred[1] * centred[1] + centred[2] * centred[2]
    flow_speed = jnp.sqrt(moving[0] * moving[0] + moving[1] * moving[1] + moving[2] * moving[2])
    thermal_energy = sites_placed(
        thermal_state, ghost_layer_sites, REFERENCE_SPOT, interior_block, interior_block
    )
    inertia = sites_placed(
        mass_per_volume, ghost_layer_sites, REFERENCE_SPOT, interior_block, interior_block
    )
    return flow_speed + jnp.sqrt(GAMMA * thermal_energy + field_square / inertia)


def edge_fields(
    interface_quantities, face_margin, bulk_motion, ghost_layer_sites, propagation_rate
):
    low_side = REFERENCE_SPOT
    high_side = (1, 1, 1)
    fields_out = []
    for edge_axis in range(3):
        first_axis = (edge_axis + 1) % 3
        second_axis = (edge_axis + 2) % 3
        back_first = unit_step(first_axis, -1)
        back_second = unit_step(second_axis, -1)
        back_both = combine_steps(back_first, back_second)

        def corner_mean(source, source_margin):
            return 0.25 * (
                sites_placed(source, source_margin, REFERENCE_SPOT, low_side, high_side)
                + sites_placed(source, source_margin, back_first, low_side, high_side)
                + sites_placed(source, source_margin, back_second, low_side, high_side)
                + sites_placed(source, source_margin, back_both, low_side, high_side)
            )

        mean_first = corner_mean(bulk_motion[first_axis], ghost_layer_sites)
        mean_second = corner_mean(bulk_motion[second_axis], ghost_layer_sites)
        mean_speed = corner_mean(propagation_rate, 1)
        first_here = sites_placed(
            interface_quantities[first_axis], face_margin, REFERENCE_SPOT, low_side, high_side
        )
        first_below = sites_placed(
            interface_quantities[first_axis], face_margin, back_second, low_side, high_side
        )
        second_here = sites_placed(
            interface_quantities[second_axis], face_margin, REFERENCE_SPOT, low_side, high_side
        )
        second_below = sites_placed(
            interface_quantities[second_axis], face_margin, back_first, low_side, high_side
        )
        fields_out.append(
            mean_second * (0.5 * (first_here + first_below))
            - mean_first * (0.5 * (second_here + second_below))
            + 0.5 * mean_speed * (second_here - second_below)
            - 0.5 * mean_speed * (first_here - first_below)
        )
    return fields_out


def edge_cells(source, offset):
    return source[
        tuple(
            (
                slice(offset[candidate], offset[candidate] + source.shape[candidate] - 1)
                for candidate in range(3)
            )
        )
    ]


def faraday(interface_quantities, face_margin, edges, interval_increment):
    renewed_result = []
    for normal in range(3):
        next_axis = (normal + 1) % 3
        last_axis = (normal + 2) % 3
        curl_part = (
            edge_cells(edges[last_axis], unit_step(next_axis, 1))
            - edge_cells(edges[last_axis], REFERENCE_SPOT)
            - (
                edge_cells(edges[next_axis], unit_step(last_axis, 1))
                - edge_cells(edges[next_axis], REFERENCE_SPOT)
            )
        )
        renewed_result.append(
            trim_extent(interface_quantities[normal], face_margin, 0)
            - interval_increment * curl_part
        )
    return jnp.stack(renewed_result)


def refresh_section(newest_iterate, subdivision_width):
    return extended(newest_iterate, (("gx", 0), ("gy", 1), ("gz", 2)), subdivision_width)


def on_device(thermal_state, diffusivity, staggered_flux_density, bulk_motion, mass_per_volume):
    subdivision_width = 2
    ghost_width = subdivision_width + 1
    bundle = jnp.concatenate(
        [
            thermal_state[None],
            diffusivity[None],
            staggered_flux_density,
            bulk_motion,
            mass_per_volume[None],
        ],
        axis=0,
    )
    extended_array = extended(bundle, (("gx", 1), ("gy", 2), ("gz", 3)), ghost_width)
    thermal_state_extended = extended_array[0]
    diffusivity_extended = extended_array[1]
    staggered_extended = extended_array[2:5]
    velocity_extended = extended_array[5:8]
    mass_per_volume_extended = extended_array[8]
    diffusion_coefficient = diffusivity_extended * jnp.power(thermal_state_extended, 2.5)
    limit_scale = (SECTIONS * SECTIONS + SECTIONS - 2) / 16.0
    local_step = jnp.min(limit_scale / trim_extent(diffusion_coefficient, ghost_width, 0))
    interval_increment = lax.pmin(local_step, ("gx", "gy", "gz"))
    propagation_rate = fastest_characteristic(
        thermal_state_extended,
        mass_per_volume_extended,
        staggered_extended,
        velocity_extended,
        ghost_width,
    )
    edges_now = edge_fields(
        staggered_extended, ghost_width, velocity_extended, ghost_width, propagation_rate
    )
    faces_mid = faraday(staggered_extended, ghost_width, edges_now, interval_increment)
    mid_margin = 0
    faces_mid_pad = extended(faces_mid, (("gx", 1), ("gy", 2), ("gz", 3)), 1)
    mid_margin = 1
    lookup_arrays = face_coefficients(
        diffusion_coefficient, staggered_extended, ghost_width, subdivision_width
    )
    initial_derivative = diffuse_thermal(
        thermal_state_extended, ghost_width, lookup_arrays, subdivision_width, subdivision_width - 1
    )
    layout_recipe = section_weights(SECTIONS)
    previous_iterate, previous_extended = (thermal_state_extended, ghost_width)
    newest_iterate = (
        trim_extent(thermal_state_extended, ghost_width, subdivision_width - 1)
        + layout_recipe[1] * interval_increment * initial_derivative
    )
    newest_extended = subdivision_width - 1
    for subdivision_number in range(2, SECTIONS + 1):
        if newest_extended == 0:
            if subdivision_number == subdivision_width + 1:
                newest_iterate = refresh_section(newest_iterate, subdivision_width)
            else:
                newest_iterate = refresh_section(newest_iterate, subdivision_width)
            newest_extended = subdivision_width
        renewed_result = subdivision_advance(
            layout_recipe[subdivision_number],
            interval_increment,
            newest_iterate,
            newest_extended,
            previous_iterate,
            previous_extended,
            thermal_state_extended,
            ghost_width,
            initial_derivative,
            subdivision_width - 1,
            lookup_arrays,
            subdivision_width,
        )
        previous_iterate, previous_extended = (newest_iterate, newest_extended)
        newest_iterate, newest_extended = (renewed_result, newest_extended - 1)
    edges_mid = edge_fields(
        faces_mid_pad, mid_margin, velocity_extended, ghost_width, propagation_rate
    )
    faces_end = faraday(faces_mid_pad, mid_margin, edges_mid, interval_increment)
    face_out = 0.5 * (trim_extent(staggered_extended, ghost_width, 0) + faces_end)
    return (newest_iterate, face_out)


def solution(mesh):
    return jax.shard_map(
        on_device,
        mesh=mesh,
        in_specs=(
            P("gx", "gy", "gz"),
            P("gx", "gy", "gz"),
            P(None, "gx", "gy", "gz"),
            P(None, "gx", "gy", "gz"),
            P("gx", "gy", "gz"),
        ),
        out_specs=(P("gx", "gy", "gz"), P(None, "gx", "gy", "gz")),
        check_vma=False,
    )
```

profile of v0, /device:TPU:1, one launch (start us, length us, event | category | flops | bytes accessed | tf_op | source)
XLA Modules:
  0.0 195.3 jit_solution(14155555475665759196)
XLA Ops:
  2.2 0.9 constant_dynamic-update-slice_fusion.1
  3.1 0.9 constant_dynamic-update-slice_fusion
  4.7 2.7 %collective-permute-start = (f32[9,3,8,128]{3,2,1,0:T(8,128)S(1)}, f32[9,3,8,128]{3,2,1,0:T(8,128)S(1)}, u32[]{:S(2)}, u32[]{:S(2)}) collective-permute-start(f32[9,3,8,128]{3,2,1,0:T(8,128)S(1)} %get-tuple-element.45), channel_id=1, source_target_pairs={{0,8},{8,16},{16,24},{24,0},{1,9},{9,17},{17,25},{25,1},{2,10},{10... | collective-permute-start | bytes 331784 | tf_op jit(solution)/shard_map/ppermute | solution.py:20
  7.4 2.8 %collective-permute-done = f32[9,3,8,128]{3,2,1,0:T(8,128)S(1)} collective-permute-done((f32[9,3,8,128]{3,2,1,0:T(8,128)S(1)}, f32[9,3,8,128]{3,2,1,0:T(8,128)S(1)}, u32[]{:S(2)}, u32[]{:S(2)}) %collective-permute-start) | collective-permute-done | bytes 110624 | tf_op jit(solution)/shard_map/ppermute | solution.py:20
  10.2 1.4 collective-permute-done.1
  11.7 1.3 collective-permute-start.2
  13.4 5.5 %copy.32 = f32[9,14,8,128]{2,1,3,0:T(8,128)} copy(f32[9,14,8,128]{3,2,1,0:T(8,128)S(1)} %pad_maximum_fusion.2) | data formatting | bytes 1032192 | tf_op jit(solution)/shard_map/concatenate | solution.py:24
  19.2 5.4 %copy.31 = f32[9,14,3,128]{2,1,3,0:T(8,128)} copy(f32[9,14,3,128]{3,1,2,0:T(8,128)S(1)} %collective-permute-done.2) | data formatting | bytes 387072 | tf_op jit(solution)/shard_map/ppermute | solution.py:20
  24.7 5.5 %copy.33 = f32[9,14,3,128]{2,1,3,0:T(8,128)} copy(f32[9,14,3,128]{3,1,2,0:T(8,128)S(1)} %collective-permute-done.3) | data formatting | bytes 387072 | tf_op jit(solution)/shard_map/ppermute | solution.py:23
  30.1 11.1 %pad_maximum_fusion = f32[9,14,14,128]{2,1,3,0:T(8,128)S(1)} fusion(f32[9,14,3,128]{2,1,3,0:T(8,128)} %copy.33, f32[9,14,8,128]{2,1,3,0:T(8,128)} %copy.32, f32[9,14,3,128]{2,1,3,0:T(8,128)} %copy.31), kind=kLoop, calls=%fused_computation | loop fusion | flops 451584 | bytes 1806336 | tf_op jit(solution)/shard_map/concatenate | solution.py:24
  41.2 3.6 %copy-done = f32[9,14,14,128]{2,1,3,0:T(8,128)} copy-done((f32[9,14,14,128]{2,1,3,0:T(8,128)}, f32[9,14,14,128]{2,1,3,0:T(8,128)S(1)}, u32[]{:S(2)}) %copy-start) | copy-done | bytes 903192
  44.9 3.4 %collective-permute-start.5 = (f32[9,14,14,3]{2,1,3,0:T(8,128)S(1)}, f32[9,14,14,3]{2,1,3,0:T(8,128)S(1)}, u32[]{:S(2)}, u32[]{:S(2)}) collective-permute-start(f32[9,14,14,3]{2,1,3,0:T(8,128)S(1)} %get-tuple-element.31), channel_id=1, source_target_pairs={{1,0},{2,1},{3,2},{0,3},{5,4},{6,5},{7,6},{4,7},{9,8},{10,9},{11,1... | collective-permute-start | bytes 63512 | tf_op jit(solution)/shard_map/ppermute | solution.py:23
  48.3 6.5 %copy.35 = f32[9,14,14,128]{3,2,1,0:T(8,128)S(1)} copy(f32[9,14,14,128]{2,1,3,0:T(8,128)} %copy-done) | data formatting | bytes 1806336 | tf_op jit(solution)/shard_map/concatenate | solution.py:24
  55.7 3.4 %collective-permute-done.4 = f32[9,14,14,3]{2,1,3,0:T(8,128)S(1)} collective-permute-done((f32[9,14,14,3]{2,1,3,0:T(8,128)S(1)}, f32[9,14,14,3]{2,1,3,0:T(8,128)S(1)}, u32[]{:S(2)}, u32[]{:S(2)}) %collective-permute-start.4) | collective-permute-done | bytes 21200 | tf_op jit(solution)/shard_map/ppermute | solution.py:20
  62.6 1.3 slice_multiply_fusion.1
  63.9 1.3 slice_multiply_fusion.2
  65.2 1.2 slice_multiply_fusion
  66.4 38.8 %pmin.7 = f32[]{:T(128)} all-reduce(f32[]{:T(128)} %fusion.318), channel_id=1, replica_groups=mesh['gx'=4,'gy'=2,'gz'=4] {'gx','gy','gz'}, use_global_device_ids=true, to_apply=%region_1.0 | all-reduce | flops 1 | bytes 8 | tf_op jit(solution)/shard_map/pmin | solution.py:365
  105.9 1.0 fusion.343
  106.9 1.0 fusion.342
  109.2 1.2 fusion.344
  110.9 2.2 %multiply_add_fusion = (f32[10,10,130]{2,1,0:T(8,128)S(1)}, f32[10,10,130]{2,1,0:T(8,128)}, f32[10,10,130]{2,1,0:T(8,128)S(1)}) fusion(f32[14,14,134]{2,1,0:T(8,128)S(1)} %get-tuple-element.39, f32[]{:T(128)S(6)} %mul_shard_map.45, f32[10,10,131]{2,1,0:T(8,128)S(1)} %fusion.138, f32[10,11,130]{2,1,0:T(8,128)S(1)} %fusion.147, ...), kind=kLoop, calls=%fused_computation.305 | loop fusion | flops 364000 | bytes 1040004 | tf_op jit(solution)/shard_map/add | solution.py:389
  115.6 1.4 multiply_subtract_fusion.4
  117.1 1.4 multiply_subtract_fusion.3
  118.5 1.5 multiply_subtract_fusion.5
  121.3 1.2 fusion.313
  122.5 3.4 %collective-permute-start.6 = (f32[2,8,128]{2,1,0:T(8,128)S(1)}, f32[2,8,128]{2,1,0:T(8,128)S(1)}, u32[]{:S(2)}, u32[]{:S(2)}) collective-permute-start(f32[2,8,128]{2,1,0:T(8,128)S(1)} %get-tuple-element.90), channel_id=1, source_target_pairs={{0,8},{8,16},{16,24},{24,0},{1,9},{9,17},{17,25},{25,1},{2,10},{10... | collective-permute-start | bytes 24584 | tf_op jit(solution)/shard_map/ppermute | solution.py:20
  125.9 1.8 fusion.285
  135.5 1.8 collective-permute-start.24
  137.4 1.2 collective-permute-start.8
  138.9 1.8 collective-permute-done.25
  141.4 3.1 %collective-permute-start.11 = (f32[12,12,2]{2,1,0:T(8,128)S(1)}, f32[12,12,2]{2,1,0:T(8,128)S(1)}, u32[]{:S(2)}, u32[]{:S(2)}) collective-permute-start(f32[12,12,2]{2,1,0:T(8,128)S(1)} %get-tuple-element.73), channel_id=1, source_target_pairs={{1,0},{2,1},{3,2},{0,3},{5,4},{6,5},{7,6},{4,7},{9,8},{10,9},{11,1... | collective-permute-start | bytes 3464 | tf_op jit(solution)/shard_map/ppermute | solution.py:23
  145.2 0.9 collective-permute-start.26
  148.3 1.1 fusion.113
  150.6 3.6 %collective-permute-start.29 = (f32[3,10,10,1]{3,0,2,1:T(4,128)S(1)}, f32[3,10,10,1]{3,0,2,1:T(4,128)S(1)}, u32[]{:S(2)}, u32[]{:S(2)}) collective-permute-start(f32[3,10,10,1]{3,0,2,1:T(4,128)S(1)} %get-tuple-element.49), channel_id=1, source_target_pairs={{1,0},{2,1},{3,2},{0,3},{5,4},{6,5},{7,6},{4,7},{9,8},{10,9},{11,1... | collective-permute-start | bytes 3608 | tf_op jit(solution)/shard_map/ppermute | solution.py:23
  154.3 4.6 %collective-permute-start.12 = (f32[2,8,128]{2,1,0:T(8,128)S(1)}, f32[2,8,128]{2,1,0:T(8,128)S(1)}, u32[]{:S(2)}, u32[]{:S(2)}) collective-permute-start(f32[2,8,128]{2,1,0:T(8,128)S(1)} %get-tuple-element.88), channel_id=1, source_target_pairs={{0,8},{8,16},{16,24},{24,0},{1,9},{9,17},{17,25},{25,1},{2,10},{10... | collective-permute-start | bytes 24584 | tf_op jit(solution)/shard_map/ppermute | solution.py:20
  159.2 1.0 pad_maximum_fusion.13
  160.2 2.0 %collective-permute-done.13 = f32[2,8,128]{2,1,0:T(8,128)S(1)} collective-permute-done((f32[2,8,128]{2,1,0:T(8,128)S(1)}, f32[2,8,128]{2,1,0:T(8,128)S(1)}, u32[]{:S(2)}, u32[]{:S(2)}) %collective-permute-start.13) | collective-permute-done | bytes 8224 | tf_op jit(solution)/shard_map/ppermute | solution.py:23
  162.6 1.1 collective-permute-start.15
  163.8 1.0 collective-permute-done.14
  165.3 2.3 %collective-permute-start.16 = (f32[12,12,2]{2,1,0:T(8,128)S(1)}, f32[12,12,2]{2,1,0:T(8,128)S(1)}, u32[]{:S(2)}, u32[]{:S(2)}) collective-permute-start(f32[12,12,2]{2,1,0:T(8,128)S(1)} %get-tuple-element.70), channel_id=1, source_target_pairs={{0,1},{1,2},{2,3},{3,0},{4,5},{5,6},{6,7},{7,4},{8,9},{9,10},{10,1... | collective-permute-start | bytes 3464 | tf_op jit(solution)/shard_map/ppermute | solution.py:20
  167.6 1.0 collective-permute-start.17
  168.6 1.4 multiply_subtract_fusion.2
  170.7 1.0 collective-permute-done.17
  174.4 5.4 %collective-permute-start.18 = (f32[2,8,128]{2,1,0:T(8,128)S(1)}, f32[2,8,128]{2,1,0:T(8,128)S(1)}, u32[]{:S(2)}, u32[]{:S(2)}) collective-permute-start(f32[2,8,128]{2,1,0:T(8,128)S(1)} %get-tuple-element.86), channel_id=1, source_target_pairs={{0,8},{8,16},{16,24},{24,0},{1,9},{9,17},{17,25},{25,1},{2,10},{10... | collective-permute-start | bytes 24584 | tf_op jit(solution)/shard_map/ppermute | solution.py:20
  180.6 2.3 %collective-permute-done.19 = f32[2,8,128]{2,1,0:T(8,128)S(1)} collective-permute-done((f32[2,8,128]{2,1,0:T(8,128)S(1)}, f32[2,8,128]{2,1,0:T(8,128)S(1)}, u32[]{:S(2)}, u32[]{:S(2)}) %collective-permute-start.19) | collective-permute-done | bytes 8224 | tf_op jit(solution)/shard_map/ppermute | solution.py:23
  186.8 3.0 %collective-permute-start.23 = (f32[12,12,2]{2,1,0:T(8,128)S(1)}, f32[12,12,2]{2,1,0:T(8,128)S(1)}, u32[]{:S(2)}, u32[]{:S(2)}) collective-permute-start(f32[12,12,2]{2,1,0:T(8,128)S(1)} %get-tuple-element.69), channel_id=1, source_target_pairs={{1,0},{2,1},{3,2},{0,3},{5,4},{6,5},{7,6},{4,7},{9,8},{10,9},{11,1... | collective-permute-start | bytes 3464 | tf_op jit(solution)/shard_map/ppermute | solution.py:23
  190.4 1.5 collective-permute-done.22
  (127 shorter events, 30.2 us)
Async XLA Ops:
  4.7 5.5 %collective-permute-start = (f32[9,3,8,128]{3,2,1,0:T(8,128)S(1)}, f32[9,3,8,128]{3,2,1,0:T(8,128)S(1)}, u32[]{:S(2)}, u32[]{:S(2)}) collective-permute-start(f32[9,3,8,128]{3,2,1,0:T(8,128)S(1)} %get-tuple-element.45), channel_id=1, source_target_pairs={{0,8},{8,16},{16,24},{24,0},{1,9},{9,17},{17,25},{25,1},{2,10},{10... | collective-permute-start | bytes 331784 | tf_op jit(solution)/shard_map/ppermute | solution.py:20
  7.4 4.2 %collective-permute-start.1 = (f32[9,3,8,128]{3,2,1,0:T(8,128)S(1)}, f32[9,3,8,128]{3,2,1,0:T(8,128)S(1)}, u32[]{:S(2)}, u32[]{:S(2)}) collective-permute-start(f32[9,3,8,128]{3,2,1,0:T(8,128)S(1)} %get-tuple-element.46), channel_id=1, source_target_pairs={{8,0},{16,8},{24,16},{0,24},{9,1},{17,9},{25,17},{1,25},{10,2},{18... | collective-permute-start | bytes 331784 | tf_op jit(solution)/shard_map/ppermute | solution.py:23
  11.7 7.5 %collective-permute-start.2 = (f32[9,14,3,128]{3,1,2,0:T(8,128)S(1)}, f32[9,14,3,128]{3,1,2,0:T(8,128)S(1)}, u32[]{:S(2)}, u32[]{:S(2)}) collective-permute-start(f32[9,14,3,128]{3,1,2,0:T(8,128)S(1)} %copy.43), channel_id=1, source_target_pairs={{0,4},{4,0},{1,5},{5,1},{2,6},{6,2},{3,7},{7,3},{8,12},{12,8},{9,1... | collective-permute-start | bytes 580616 | tf_op jit(solution)/shard_map/ppermute | solution.py:20
  13.0 11.6 %collective-permute-start.3 = (f32[9,14,3,128]{3,1,2,0:T(8,128)S(1)}, f32[9,14,3,128]{3,1,2,0:T(8,128)S(1)}, u32[]{:S(2)}, u32[]{:S(2)}) collective-permute-start(f32[9,14,3,128]{3,1,2,0:T(8,128)S(1)} %copy.44), channel_id=1, source_target_pairs={{4,0},{0,4},{5,1},{1,5},{6,2},{2,6},{7,3},{3,7},{12,8},{8,12},{13,... | collective-permute-start | bytes 580616 | tf_op jit(solution)/shard_map/ppermute | solution.py:23
  41.2 3.7 %copy-start = (f32[9,14,14,128]{2,1,3,0:T(8,128)}, f32[9,14,14,128]{2,1,3,0:T(8,128)S(1)}, u32[]{:S(2)}) copy-start(f32[9,14,14,128]{2,1,3,0:T(8,128)S(1)} %pad_maximum_fusion) | copy-start | bytes 2709508
  44.9 9.9 %collective-permute-start.5 = (f32[9,14,14,3]{2,1,3,0:T(8,128)S(1)}, f32[9,14,14,3]{2,1,3,0:T(8,128)S(1)}, u32[]{:S(2)}, u32[]{:S(2)}) collective-permute-start(f32[9,14,14,3]{2,1,3,0:T(8,128)S(1)} %get-tuple-element.31), channel_id=1, source_target_pairs={{1,0},{2,1},{3,2},{0,3},{5,4},{6,5},{7,6},{4,7},{9,8},{10,9},{11,1... | collective-permute-start | bytes 63512 | tf_op jit(solution)/shard_map/ppermute | solution.py:23
  48.3 10.8 %collective-permute-start.4 = (f32[9,14,14,3]{2,1,3,0:T(8,128)S(1)}, f32[9,14,14,3]{2,1,3,0:T(8,128)S(1)}, u32[]{:S(2)}, u32[]{:S(2)}) collective-permute-start(f32[9,14,14,3]{2,1,3,0:T(8,128)S(1)} %get-tuple-element.30), channel_id=1, source_target_pairs={{0,1},{1,2},{2,3},{3,0},{4,5},{5,6},{6,7},{7,4},{8,9},{9,10},{10,1... | collective-permute-start | bytes 63512 | tf_op jit(solution)/shard_map/ppermute | solution.py:20
  118.5 31.6 %copy-start.1 = (f32[10,10,130]{2,1,0:T(8,128)S(1)}, f32[10,10,130]{2,1,0:T(8,128)}, u32[]{:S(2)}) copy-start(f32[10,10,130]{2,1,0:T(8,128)} %get-tuple-element.17) | copy-start | bytes 156004
  122.5 14.8 %collective-permute-start.6 = (f32[2,8,128]{2,1,0:T(8,128)S(1)}, f32[2,8,128]{2,1,0:T(8,128)S(1)}, u32[]{:S(2)}, u32[]{:S(2)}) collective-permute-start(f32[2,8,128]{2,1,0:T(8,128)S(1)} %get-tuple-element.90), channel_id=1, source_target_pairs={{0,8},{8,16},{16,24},{24,0},{1,9},{9,17},{17,25},{25,1},{2,10},{10... | collective-permute-start | bytes 24584 | tf_op jit(solution)/shard_map/ppermute | solution.py:20
  125.9 11.4 %collective-permute-start.7 = (f32[2,8,128]{2,1,0:T(8,128)S(1)}, f32[2,8,128]{2,1,0:T(8,128)S(1)}, u32[]{:S(2)}, u32[]{:S(2)}) collective-permute-start(f32[2,8,128]{2,1,0:T(8,128)S(1)} %get-tuple-element.91), channel_id=1, source_target_pairs={{8,0},{16,8},{24,16},{0,24},{9,1},{17,9},{25,17},{1,25},{10,2},{18... | collective-permute-start | bytes 24584 | tf_op jit(solution)/shard_map/ppermute | solution.py:23
  127.7 40.9 %copy-start.5 = (f32[9,9,129]{2,1,0:T(8,128)S(1)}, f32[9,9,129]{2,1,0:T(8,128)}, u32[]{:S(2)}) copy-start(f32[9,9,129]{2,1,0:T(8,128)} %get-tuple-element.5) | copy-start | bytes 125392
  127.7 40.9 %copy-start.6 = (f32[9,9,129]{2,1,0:T(8,128)S(1)}, f32[9,9,129]{2,1,0:T(8,128)}, u32[]{:S(2)}) copy-start(f32[9,9,129]{2,1,0:T(8,128)} %get-tuple-element.6) | copy-start | bytes 125392
  127.7 40.9 %copy-start.7 = (f32[9,9,129]{2,1,0:T(8,128)S(1)}, f32[9,9,129]{2,1,0:T(8,128)}, u32[]{:S(2)}) copy-start(f32[9,9,129]{2,1,0:T(8,128)} %get-tuple-element.7) | copy-start | bytes 125392
  135.5 3.4 %collective-permute-start.24 = (f32[3,1,8,128]{3,2,1,0:T(8,128)S(1)}, f32[3,1,8,128]{3,2,1,0:T(8,128)S(1)}, u32[]{:S(2)}, u32[]{:S(2)}) collective-permute-start(f32[3,1,8,128]{3,2,1,0:T(8,128)S(1)} %get-tuple-element.66), channel_id=1, source_target_pairs={{0,8},{8,16},{16,24},{24,0},{1,9},{9,17},{17,25},{25,1},{2,10},{10... | collective-permute-start | bytes 36872 | tf_op jit(solution)/shard_map/ppermute | solution.py:20
  137.3 3.3 %collective-permute-start.25 = (f32[3,1,8,128]{3,2,1,0:T(8,128)S(1)}, f32[3,1,8,128]{3,2,1,0:T(8,128)S(1)}, u32[]{:S(2)}, u32[]{:S(2)}) collective-permute-start(f32[3,1,8,128]{3,2,1,0:T(8,128)S(1)} %get-tuple-element.67), channel_id=1, source_target_pairs={{8,0},{16,8},{24,16},{0,24},{9,1},{17,9},{25,17},{1,25},{10,2},{18... | collective-permute-start | bytes 36872 | tf_op jit(solution)/shard_map/ppermute | solution.py:23
  137.4 3.3 %collective-permute-start.8 = (f32[12,2,128]{2,1,0:T(2,128)S(1)}, f32[12,2,128]{2,1,0:T(2,128)S(1)}, u32[]{:S(2)}, u32[]{:S(2)}) collective-permute-start(f32[12,2,128]{2,1,0:T(2,128)S(1)} %get-tuple-element.84), channel_id=1, source_target_pairs={{0,4},{4,0},{1,5},{5,1},{2,6},{6,2},{3,7},{7,3},{8,12},{12,8},{9,1... | collective-permute-start | bytes 36872 | tf_op jit(solution)/shard_map/ppermute | solution.py:20
  138.6 2.5 %collective-permute-start.9 = (f32[12,2,128]{2,1,0:T(2,128)S(1)}, f32[12,2,128]{2,1,0:T(2,128)S(1)}, u32[]{:S(2)}, u32[]{:S(2)}) collective-permute-start(f32[12,2,128]{2,1,0:T(2,128)S(1)} %get-tuple-element.85), channel_id=1, source_target_pairs={{4,0},{0,4},{5,1},{1,5},{6,2},{2,6},{7,3},{3,7},{12,8},{8,12},{13,... | collective-permute-start | bytes 36872 | tf_op jit(solution)/shard_map/ppermute | solution.py:23
  141.2 5.3 %collective-permute-start.10 = (f32[12,12,2]{2,1,0:T(8,128)S(1)}, f32[12,12,2]{2,1,0:T(8,128)S(1)}, u32[]{:S(2)}, u32[]{:S(2)}) collective-permute-start(f32[12,12,2]{2,1,0:T(8,128)S(1)} %get-tuple-element.72), channel_id=1, source_target_pairs={{0,1},{1,2},{2,3},{3,0},{4,5},{5,6},{6,7},{7,4},{8,9},{9,10},{10,1... | collective-permute-start | bytes 3464 | tf_op jit(solution)/shard_map/ppermute | solution.py:20
  141.4 5.1 %collective-permute-start.11 = (f32[12,12,2]{2,1,0:T(8,128)S(1)}, f32[12,12,2]{2,1,0:T(8,128)S(1)}, u32[]{:S(2)}, u32[]{:S(2)}) collective-permute-start(f32[12,12,2]{2,1,0:T(8,128)S(1)} %get-tuple-element.73), channel_id=1, source_target_pairs={{1,0},{2,1},{3,2},{0,3},{5,4},{6,5},{7,6},{4,7},{9,8},{10,9},{11,1... | collective-permute-start | bytes 3464 | tf_op jit(solution)/shard_map/ppermute | solution.py:23
  144.6 5.8 %collective-permute-start.27 = (f32[3,10,1,128]{3,2,1,0:T(1,128)S(1)}, f32[3,10,1,128]{3,2,1,0:T(1,128)S(1)}, u32[]{:S(2)}, u32[]{:S(2)}) collective-permute-start(f32[3,10,1,128]{3,2,1,0:T(1,128)S(1)} %get-tuple-element.64), channel_id=1, source_target_pairs={{4,0},{0,4},{5,1},{1,5},{6,2},{2,6},{7,3},{3,7},{12,8},{8,12},{13,... | collective-permute-start | bytes 46088 | tf_op jit(solution)/shard_map/ppermute | solution.py:23
  145.2 5.1 %collective-permute-start.26 = (f32[3,10,1,128]{3,2,1,0:T(1,128)S(1)}, f32[3,10,1,128]{3,2,1,0:T(1,128)S(1)}, u32[]{:S(2)}, u32[]{:S(2)}) collective-permute-start(f32[3,10,1,128]{3,2,1,0:T(1,128)S(1)} %get-tuple-element.65), channel_id=1, source_target_pairs={{0,4},{4,0},{1,5},{5,1},{2,6},{6,2},{3,7},{7,3},{8,12},{12,8},{9,1... | collective-permute-start | bytes 46088 | tf_op jit(solution)/shard_map/ppermute | solution.py:20
  150.1 29.7 %copy-start.2 = (f32[9,9,129]{2,1,0:T(8,128)S(1)}, f32[9,9,129]{2,1,0:T(8,128)}, u32[]{:S(2)}) copy-start(f32[9,9,129]{2,1,0:T(8,128)} %get-tuple-element.13) | copy-start | bytes 125392
  150.1 29.7 %copy-start.3 = (f32[9,9,129]{2,1,0:T(8,128)S(1)}, f32[9,9,129]{2,1,0:T(8,128)}, u32[]{:S(2)}) copy-start(f32[9,9,129]{2,1,0:T(8,128)} %get-tuple-element.14) | copy-start | bytes 125392
  150.1 29.7 %copy-start.4 = (f32[9,9,129]{2,1,0:T(8,128)S(1)}, f32[9,9,129]{2,1,0:T(8,128)}, u32[]{:S(2)}) copy-start(f32[9,9,129]{2,1,0:T(8,128)} %get-tuple-element.15) | copy-start | bytes 125392
  150.6 8.3 %collective-permute-start.28 = (f32[3,10,10,1]{3,0,2,1:T(4,128)S(1)}, f32[3,10,10,1]{3,0,2,1:T(4,128)S(1)}, u32[]{:S(2)}, u32[]{:S(2)}) collective-permute-start(f32[3,10,10,1]{3,0,2,1:T(4,128)S(1)} %get-tuple-element.48), channel_id=1, source_target_pairs={{0,1},{1,2},{2,3},{3,0},{4,5},{5,6},{6,7},{7,4},{8,9},{9,10},{10,1... | collective-permute-start | bytes 3608 | tf_op jit(solution)/shard_map/ppermute | solution.py:20
  150.6 8.5 %collective-permute-start.29 = (f32[3,10,10,1]{3,0,2,1:T(4,128)S(1)}, f32[3,10,10,1]{3,0,2,1:T(4,128)S(1)}, u32[]{:S(2)}, u32[]{:S(2)}) collective-permute-start(f32[3,10,10,1]{3,0,2,1:T(4,128)S(1)} %get-tuple-element.49), channel_id=1, source_target_pairs={{1,0},{2,1},{3,2},{0,3},{5,4},{6,5},{7,6},{4,7},{9,8},{10,9},{11,1... | collective-permute-start | bytes 3608 | tf_op jit(solution)/shard_map/ppermute | solution.py:23
  154.3 5.9 %collective-permute-start.12 = (f32[2,8,128]{2,1,0:T(8,128)S(1)}, f32[2,8,128]{2,1,0:T(8,128)S(1)}, u32[]{:S(2)}, u32[]{:S(2)}) collective-permute-start(f32[2,8,128]{2,1,0:T(8,128)S(1)} %get-tuple-element.88), channel_id=1, source_target_pairs={{0,8},{8,16},{16,24},{24,0},{1,9},{9,17},{17,25},{25,1},{2,10},{10... | collective-permute-start | bytes 24584 | tf_op jit(solution)/shard_map/ppermute | solution.py:20
  158.8 3.4 %collective-permute-start.13 = (f32[2,8,128]{2,1,0:T(8,128)S(1)}, f32[2,8,128]{2,1,0:T(8,128)S(1)}, u32[]{:S(2)}, u32[]{:S(2)}) collective-permute-start(f32[2,8,128]{2,1,0:T(8,128)S(1)} %get-tuple-element.89), channel_id=1, source_target_pairs={{8,0},{16,8},{24,16},{0,24},{9,1},{17,9},{25,17},{1,25},{10,2},{18... | collective-permute-start | bytes 24584 | tf_op jit(solution)/shard_map/ppermute | solution.py:23
  160.2 29.6 %copy-start.8 = (f32[3,8,8,128]{3,2,1,0:T(8,128)S(1)}, f32[3,8,8,128]{3,2,1,0:T(8,128)}, u32[]{:S(2)}) copy-start(f32[3,8,8,128]{3,2,1,0:T(8,128)} %param.7) | copy-start | bytes 294916
  162.2 2.6 %collective-permute-start.14 = (f32[12,2,128]{2,1,0:T(2,128)S(1)}, f32[12,2,128]{2,1,0:T(2,128)S(1)}, u32[]{:S(2)}, u32[]{:S(2)}) collective-permute-start(f32[12,2,128]{2,1,0:T(2,128)S(1)} %get-tuple-element.82), channel_id=1, source_target_pairs={{0,4},{4,0},{1,5},{5,1},{2,6},{6,2},{3,7},{7,3},{8,12},{12,8},{9,1... | collective-permute-start | bytes 36872 | tf_op jit(solution)/shard_map/ppermute | solution.py:20
  162.6 2.5 %collective-permute-start.15 = (f32[12,2,128]{2,1,0:T(2,128)S(1)}, f32[12,2,128]{2,1,0:T(2,128)S(1)}, u32[]{:S(2)}, u32[]{:S(2)}) collective-permute-start(f32[12,2,128]{2,1,0:T(2,128)S(1)} %get-tuple-element.83), channel_id=1, source_target_pairs={{4,0},{0,4},{5,1},{1,5},{6,2},{2,6},{7,3},{3,7},{12,8},{8,12},{13,... | collective-permute-start | bytes 36872 | tf_op jit(solution)/shard_map/ppermute | solution.py:23
  165.3 5.4 %collective-permute-start.16 = (f32[12,12,2]{2,1,0:T(8,128)S(1)}, f32[12,12,2]{2,1,0:T(8,128)S(1)}, u32[]{:S(2)}, u32[]{:S(2)}) collective-permute-start(f32[12,12,2]{2,1,0:T(8,128)S(1)} %get-tuple-element.70), channel_id=1, source_target_pairs={{0,1},{1,2},{2,3},{3,0},{4,5},{5,6},{6,7},{7,4},{8,9},{9,10},{10,1... | collective-permute-start | bytes 3464 | tf_op jit(solution)/shard_map/ppermute | solution.py:20
  167.6 4.1 %collective-permute-start.17 = (f32[12,12,2]{2,1,0:T(8,128)S(1)}, f32[12,12,2]{2,1,0:T(8,128)S(1)}, u32[]{:S(2)}, u32[]{:S(2)}) collective-permute-start(f32[12,12,2]{2,1,0:T(8,128)S(1)} %get-tuple-element.71), channel_id=1, source_target_pairs={{1,0},{2,1},{3,2},{0,3},{5,4},{6,5},{7,6},{4,7},{9,8},{10,9},{11,1... | collective-permute-start | bytes 3464 | tf_op jit(solution)/shard_map/ppermute | solution.py:23
  174.4 6.2 %collective-permute-start.18 = (f32[2,8,128]{2,1,0:T(8,128)S(1)}, f32[2,8,128]{2,1,0:T(8,128)S(1)}, u32[]{:S(2)}, u32[]{:S(2)}) collective-permute-start(f32[2,8,128]{2,1,0:T(8,128)S(1)} %get-tuple-element.86), channel_id=1, source_target_pairs={{0,8},{8,16},{16,24},{24,0},{1,9},{9,17},{17,25},{25,1},{2,10},{10... | collective-permute-start | bytes 24584 | tf_op jit(solution)/shard_map/ppermute | solution.py:20
  179.8 3.1 %collective-permute-start.19 = (f32[2,8,128]{2,1,0:T(8,128)S(1)}, f32[2,8,128]{2,1,0:T(8,128)S(1)}, u32[]{:S(2)}, u32[]{:S(2)}) collective-permute-start(f32[2,8,128]{2,1,0:T(8,128)S(1)} %get-tuple-element.87), channel_id=1, source_target_pairs={{8,0},{16,8},{24,16},{0,24},{9,1},{17,9},{25,17},{1,25},{10,2},{18... | collective-permute-start | bytes 24584 | tf_op jit(solution)/shard_map/ppermute | solution.py:23
  182.9 2.9 %collective-permute-start.20 = (f32[12,2,128]{2,1,0:T(2,128)S(1)}, f32[12,2,128]{2,1,0:T(2,128)S(1)}, u32[]{:S(2)}, u32[]{:S(2)}) collective-permute-start(f32[12,2,128]{2,1,0:T(2,128)S(1)} %get-tuple-element.80), channel_id=1, source_target_pairs={{0,4},{4,0},{1,5},{5,1},{2,6},{6,2},{3,7},{7,3},{8,12},{12,8},{9,1... | collective-permute-start | bytes 36872 | tf_op jit(solution)/shard_map/ppermute | solution.py:20
  183.8 2.5 %collective-permute-start.21 = (f32[12,2,128]{2,1,0:T(2,128)S(1)}, f32[12,2,128]{2,1,0:T(2,128)S(1)}, u32[]{:S(2)}, u32[]{:S(2)}) collective-permute-start(f32[12,2,128]{2,1,0:T(2,128)S(1)} %get-tuple-element.81), channel_id=1, source_target_pairs={{4,0},{0,4},{5,1},{1,5},{6,2},{2,6},{7,3},{3,7},{12,8},{8,12},{13,... | collective-permute-start | bytes 36872 | tf_op jit(solution)/shard_map/ppermute | solution.py:23
  186.4 5.5 %collective-permute-start.22 = (f32[12,12,2]{2,1,0:T(8,128)S(1)}, f32[12,12,2]{2,1,0:T(8,128)S(1)}, u32[]{:S(2)}, u32[]{:S(2)}) collective-permute-start(f32[12,12,2]{2,1,0:T(8,128)S(1)} %get-tuple-element.68), channel_id=1, source_target_pairs={{0,1},{1,2},{2,3},{3,0},{4,5},{5,6},{6,7},{7,4},{8,9},{9,10},{10,1... | collective-permute-start | bytes 3464 | tf_op jit(solution)/shard_map/ppermute | solution.py:20
  186.8 5.2 %collective-permute-start.23 = (f32[12,12,2]{2,1,0:T(8,128)S(1)}, f32[12,12,2]{2,1,0:T(8,128)S(1)}, u32[]{:S(2)}, u32[]{:S(2)}) collective-permute-start(f32[12,12,2]{2,1,0:T(8,128)S(1)} %get-tuple-element.69), channel_id=1, source_target_pairs={{1,0},{2,1},{3,2},{0,3},{5,4},{6,5},{7,6},{4,7},{9,8},{10,9},{11,1... | collective-permute-start | bytes 3464 | tf_op jit(solution)/shard_map/ppermute | solution.py:23
where the time goes:
time: 199 us; the launch traced here: 195 us
  other arithmetic  47.3 us (24%)
  starting transfers between devices  42.6 us (21%)
  blocking collectives  38.8 us (19%)
  local copies, waits for them, and re-layouts  34.2 us (17%)
  waiting for transfers between devices  21.5 us (11%)
  between operations  11 us (6%)
    pmin x1, blocking collectives, on_device(): interval_increment = lax.pmin(local_step, ('gx', 'gy', 'gz'))  38.8 us
    ppermute x15, starting transfers between devices, extended(): lax.ppermute(lax.slice_in_dim(block, block.shape[dim] - width, None, axis...  25.4 us
    ppermute x15, starting transfers between devices, extended(): lax.ppermute(lax.slice_in_dim(block, 0, width, axis=dim), axis, backward)  17.2 us
    concatenate x13, other arithmetic, extended(): block = jnp.concatenate([low, block, high], axis=dim)  13.2 us
    concatenate x3, local copies, waits for them, and re-layouts, extended(): block = jnp.concatenate([low, block, high], axis=dim)  12 us
    ppermute x15, waiting for transfers between devices, extended(): lax.ppermute(lax.slice_in_dim(block, block.shape[dim] - width, None, axis...  11.5 us
    neg x24, other arithmetic, diffuse_thermal(): -(along_normal * (shifted(REFERENCE_SPOT) - shifted(backward)) + along_fi...  10.4 us
    ppermute x15, waiting for transfers between devices, extended(): lax.ppermute(lax.slice_in_dim(block, 0, width, axis=dim), axis, backward)  10 us
  transfers between devices with their start and end apart: 30, of which 18 were waited for; matrix products, arithmetic and copies ran while one was open for 14% of the time, Pallas kernels for 0%

commit v1 on v0

v1 whole, which is shorter than its diff:
```python
import functools
import operator

import jax
import jax.numpy as jnp
from jax import lax
from jax.experimental import pallas as pl
from jax.experimental.pallas import tpu as pltpu
from jax.sharding import PartitionSpec as P

SECTIONS = 8
GAMMA = 5.0 / 3.0
FACE_FLOOR = 0.25
MESH = pl.DeviceIdType.MESH
AXES = ("gx", "gy", "gz")
ROWS = 8
LANES = 128
WIDE = SECTIONS
THIN = 4
NWIDE = 5
NTHIN = 4


def section_weights(total):
    first_rate = 4.0 / (total * total + total - 2)
    factors = [1.0 / 3.0, 1.0 / 3.0, 1.0 / 3.0]
    for j in range(3, total + 1):
        factors.append((j * j + j - 2) / (2.0 * j * (j + 1)))
    recipe = [None, factors[1] * first_rate]
    for j in range(2, total + 1):
        p = (2.0 * j - 1.0) / j * factors[j] / factors[j - 1]
        r = -(j - 1.0) / j * factors[j] / factors[j - 2]
        m = p * first_rate
        h = -(1.0 - factors[j - 1]) * m
        recipe.append((p, r, 1.0 - p - r, m, h))
    return recipe


class Sheet:
    def __init__(self, parts):
        self.parts = parts

    def _with(self, other, op):
        if isinstance(other, Sheet):
            return Sheet([[op(a, b) for a, b in zip(p, q)] for p, q in zip(self.parts, other.parts)])
        return Sheet([[op(a, other) for a in p] for p in self.parts])

    def __add__(self, other):
        return self._with(other, operator.add)

    def __sub__(self, other):
        return self._with(other, operator.sub)

    def __mul__(self, other):
        return self._with(other, operator.mul)

    def __truediv__(self, other):
        return self._with(other, operator.truediv)

    def map(self, fn):
        return Sheet([[fn(a) for a in p] for p in self.parts])

    def y(self, step):
        n = len(self.parts)
        row = lax.broadcasted_iota(jnp.int32, (ROWS, LANES), 0)
        edge = row == (ROWS - 1 if step > 0 else 0)
        rolled = [[pltpu.roll(a, (-step) % ROWS, 0) for a in p] for p in self.parts]
        return Sheet(
            [
                [jnp.where(edge, b, a) for a, b in zip(rolled[c], rolled[(c + step) % n])]
                for c in range(n)
            ]
        )

    def z(self, step):
        lane = lax.broadcasted_iota(jnp.int32, (ROWS, LANES), 1)
        edge = lane == (LANES - 1 if step > 0 else 0)
        out = []
        for p in self.parts:
            a, b = [pltpu.roll(v, (-step) % LANES, 1) for v in p]
            out.append([jnp.where(edge, b, a), jnp.where(edge, a, b)])
        return Sheet(out)


def sqrt(sheet):
    return sheet.map(jnp.sqrt)


def get(ref, i):
    return Sheet([[ref[yc, zc, i] for zc in range(2)] for yc in range(ref.shape[0])])


def put(ref, i, sheet):
    for yc, p in enumerate(sheet.parts):
        for zc, v in enumerate(p):
            ref[yc, zc, i] = v


def flat(*sheets):
    return tuple(v for s in sheets for p in s.parts for v in p)


def unflat(values, nyc):
    size = 2 * nyc
    out = []
    for k in range(0, len(values), size):
        part = values[k : k + size]
        out.append(Sheet([list(part[2 * c : 2 * c + 2]) for c in range(nyc)]))
    return out


def centre(field):
    if field < NWIDE:
        return 2 * WIDE * field + WIDE
    return 2 * WIDE * NWIDE + 2 * THIN * (field - NWIDE) + THIN


def kernel(
    sizes, nx,
    t_in, d_in, b_in, v_in, r_in,
    t_out, b_out,
    fields, packed, mine, ends, kmax, parts_x, parts_y, parts_z,
    kappa, coef, ya, yb, rate0, speed, means, edges, mid,
    load_sem, red_send, red_recv, z_send, z_recv, y_send, y_recv, x_send, x_recv,
):
    counts = dict(zip(AXES, sizes))
    nyc = fields.shape[1]
    own = pl.ds(nx, nx)
    me = {a: lax.axis_index(a) for a in AXES}

    def at(axis, step):
        n = counts[axis]
        return {axis: lax.rem(me[axis] + (step % n), n)}

    def remote(src, dst, send, recv, device):
        return pltpu.make_async_remote_copy(
            src_ref=src, dst_ref=dst, send_sem=send, recv_sem=recv,
            device_id=device, device_id_type=MESH,
        )

    loads = [
        pltpu.make_async_copy(src, dst, load_sem.at[k])
        for k, (src, dst) in enumerate(
            (
                (t_in, fields.at[0, 0, 0, own]),
                (d_in, fields.at[1, 0, 0, own]),
                (b_in, fields.at[2:5, 0, 0, own]),
                (v_in, fields.at[5:8, 0, 0, own]),
                (r_in, fields.at[8, 0, 0, own]),
            )
        )
    ]
    for c in loads:
        c.start()
    barrier = pltpu.get_barrier_semaphore()
    greeted = 0
    for axis in AXES:
        for k in range(1, counts[axis]):
            pl.semaphore_signal(barrier, inc=1, device_id=at(axis, k), device_id_type=MESH)
            greeted += 1
    for c in loads:
        c.wait()

    lane = lax.broadcasted_iota(jnp.int32, (ROWS, LANES), 1)
    top = None
    for i in range(nx):
        t = fields[0, 0, 0, nx + i]
        k = fields[1, 0, 0, nx + i] * (t * t * jnp.sqrt(t))
        top = k if top is None else jnp.maximum(top, k)
    kmax[0] = top
    for i in range(nx):
        row = pltpu.roll(fields[0, 0, 0, nx + i], centre(0), 1)
        for f in range(1, NWIDE + NTHIN):
            start = centre(f) - (WIDE if f < NWIDE else THIN)
            row = jnp.where(lane >= start, pltpu.roll(fields[f, 0, 0, nx + i], centre(f), 1), row)
        mine[i] = row
    pl.semaphore_wait(barrier, greeted)

    sends = []

    def go(copies):
        for c in copies:
            c.start()
        sends.extend(copies)
        return copies

    slot = [0]

    def reduce_round(axis, src, dst):
        copies = []
        for k in range(1, counts[axis]):
            s = slot[0]
            slot[0] += 1
            copies.append(
                remote(src, dst.at[k - 1], red_send.at[s], red_recv.at[s], at(axis, k))
            )
        return copies

    def y_copies(s, ref):
        if nyc == 2:
            return [remote(ref(0), ref(1), y_send.at[s, 0], y_recv.at[s, 0], at("gy", 1))]
        return [
            remote(ref(0), ref(2), y_send.at[s, 0], y_recv.at[s, 0], at("gy", 1)),
            remote(ref(0), ref(1), y_send.at[s, 1], y_recv.at[s, 1], at("gy", -1)),
        ]

    def x_copies(s, ref, width):
        return [
            remote(
                ref(pl.ds(2 * nx - width, width)), ref(pl.ds(nx - width, width)),
                x_send.at[s, 0], x_recv.at[s, 0], at("gx", 1),
            ),
            remote(
                ref(pl.ds(nx, width)), ref(pl.ds(2 * nx, width)),
                x_send.at[s, 1], x_recv.at[s, 1], at("gx", -1),
            ),
        ]

    rest = pl.ds(1, nyc - 1)
    wide = pl.ds(0, NWIDE)
    thin = pl.ds(NWIDE, NTHIN)

    red_y = go(reduce_round("gy", kmax.at[0], parts_y))
    z_ends = go(
        [
            remote(mine, ends.at[0], z_send.at[0], z_recv.at[0], at("gz", 1)),
            remote(mine, ends.at[1], z_send.at[1], z_recv.at[1], at("gz", -1)),
        ]
    )
    y_wide = go(y_copies(0, lambda c: fields.at[wide, c, 0, own]))
    x_wide = go(x_copies(0, lambda r: fields.at[wide, 0, 0, r], nx))

    for c in red_y:
        c.wait_recv()
    for k in range(counts["gy"] - 1):
        top = jnp.maximum(top, parts_y[k])
    kmax[1] = top
    for c in z_ends:
        c.wait_recv()
    in_wide = lane < 2 * WIDE * NWIDE
    upper = jnp.where(in_wide, lane % (2 * WIDE) - WIDE, lane % (2 * THIN) - THIN) >= 0
    for i in range(nx):
        packed[0, nx + i] = jnp.where(upper, ends[1, i], ends[0, i])
    red_z = go(reduce_round("gz", kmax.at[1], parts_z))
    y_pack = go(y_copies(1, lambda c: packed.at[c, own]))
    y_thin = go(y_copies(2, lambda c: fields.at[thin, c, 0, own]))
    x_pack = go(x_copies(1, lambda r: packed.at[0, r], nx))

    for c in red_z:
        c.wait_recv()
    for k in range(counts["gz"] - 1):
        top = jnp.maximum(top, parts_z[k])
    kmax[2] = top
    for c in y_wide:
        c.wait_recv()
    red_x = go(reduce_round("gx", kmax.at[2], parts_x))
    x_wide2 = go(x_copies(2, lambda r: fields.at[wide, rest, 0, r], nx))
    for c in y_pack:
        c.wait_recv()
    x_pack2 = go(x_copies(3, lambda r: packed.at[rest, r], nx))
    x_thin = go(x_copies(4, lambda r: fields.at[thin, 0, 0, r], THIN))
    for c in y_thin:
        c.wait_recv()
    x_thin2 = go(x_copies(5, lambda r: fields.at[thin, rest, 0, r], THIN))
    for c in x_wide + x_pack + x_wide2 + x_pack2:
        c.wait_recv()

    def unpack(i, carry):
        for yc in range(nyc):
            pk = packed[yc, i]
            for f in range(NWIDE):
                fields[f, yc, 1, i] = pltpu.roll(pk, LANES - centre(f), 1)
            for zc in range(2):
                t = fields[0, yc, zc, i]
                kappa[yc, zc, i] = fields[1, yc, zc, i] * (t * t * jnp.sqrt(t))
        return carry

    lax.fori_loop(0, 3 * nx, unpack, 0)

    bx, by, bz = fields.at[2], fields.at[3], fields.at[4]
    t0 = fields.at[0]
    last = 3 * nx - 1

    def coefficients(i, carry):
        k0, km = get(kappa, i), get(kappa, i - 1)
        x0, xp = get(bx, i), get(bx, jnp.minimum(i + 1, last))
        y0, ym = get(by, i), get(by, i - 1)
        z0, zm = get(bz, i), get(bz, i - 1)

        def store(n, kf, bn, bo1, bo2):
            q = (bn * bn + bo1 * bo1 + bo2 * bo2).map(lambda v: jnp.maximum(v, FACE_FLOOR))
            s = kf / q * bn
            put(coef.at[3 * n], i, s * bn)
            put(coef.at[3 * n + 1], i, s * bo1 * 0.25)
            put(coef.at[3 * n + 2], i, s * bo2 * 0.25)

        sy, sz = y0 + ym, z0 + zm
        store(0, (k0 + km) * 0.5, x0, (sy + sy.y(1)) * 0.25, (sz + sz.z(1)) * 0.25)
        xx = x0 + xp
        zz = z0 + z0.z(1)
        store(1, (k0 + k0.y(-1)) * 0.5, y0, (zz + zz.y(-1)) * 0.25, (xx + xx.y(-1)) * 0.25)
        yy = y0 + y0.y(1)
        store(2, (k0 + k0.z(-1)) * 0.5, z0, (xx + xx.z(-1)) * 0.25, (yy + yy.z(-1)) * 0.25)
        return carry

    lax.fori_loop(1, 3 * nx, coefficients, 0)

    def conduct(u, reach, finish):
        def ahead(i, u0, u1, dy0, dz0):
            u1ym, u1zm = u1.y(-1), u1.z(-1)
            dy1, dz1 = u1.y(1) - u1ym, u1.z(1) - u1zm
            if u0 is None:
                return u1ym, u1zm, dy1, dz1, None
            gx = (
                get(coef.at[0], i) * (u1 - u0)
                + get(coef.at[1], i) * (dy1 + dy0)
                + get(coef.at[2], i) * (dz1 + dz0)
            )
            return u1ym, u1zm, dy1, dz1, gx

        first = nx - reach
        um, u0 = get(u, first - 1), get(u, first)
        _, _, dym, dzm, _ = ahead(first - 1, None, um, None, None)
        u0ym, u0zm, dy0, dz0, gx0 = ahead(first, um, u0, dym, dzm)

        def step(i, carry):
            um, u0, u0ym, u0zm, dy0, dz0, gx0 = unflat(carry, nyc)
            u1 = get(u, i + 1)
            u1ym, u1zm, dy1, dz1, gx1 = ahead(i + 1, u0, u1, dy0, dz0)
            dx = u1 - um
            gy = (
                get(coef.at[3], i) * (u0 - u0ym)
                + get(coef.at[4], i) * (dz0 + dz0.y(-1))
                + get(coef.at[5], i) * (dx + dx.y(-1))
            )
            gz = (
                get(coef.at[6], i) * (u0 - u0zm)
                + get(coef.at[7], i) * (dx + dx.z(-1))
                + get(coef.at[8], i) * (dy0 + dy0.z(-1))
            )
            finish(i, u0, (gx1 - gx0) + (gy.y(1) - gy) + (gz.z(1) - gz))
            return flat(u0, u1, u1ym, u1zm, dy1, dz1, gx1)

        lax.fori_loop(first, 2 * nx + reach, step, flat(um, u0, u0ym, u0zm, dy0, dz0, gx0))

    for c in red_x:
        c.wait_recv()
    for k in range(counts["gx"] - 1):
        top = jnp.maximum(top, parts_x[k])
    limit = (SECTIONS * SECTIONS + SECTIONS - 2) / 16.0
    peak = jnp.max(jnp.max(top, axis=0, keepdims=True), axis=1, keepdims=True)
    dt = jnp.broadcast_to(limit / peak, (ROWS, LANES))

    recipe = section_weights(SECTIONS)

    def begin(i, u0, rate):
        rate = rate * dt
        put(rate0, i, rate)
        put(ya, i, u0 + rate * recipe[1])

    conduct(t0, SECTIONS - 1, begin)
    newest, older = ya, yb
    for j in range(2, SECTIONS + 1):
        p, r, q, m, h = recipe[j]
        m_dt = dt * m
        prev2 = t0 if j == 2 else older

        def advance(i, u0, rate):
            value = (
                u0 * p + get(prev2, i) * r + get(t0, i) * q + rate * m_dt + get(rate0, i) * h
            )
            if j == SECTIONS:
                t_out[i - nx] = value.parts[0][0]
            else:
                put(older, i, value)

        conduct(newest, SECTIONS - j, advance)
        newest, older = older, newest

    for c in x_thin + x_thin2:
        c.wait_recv()
    vx, vy, vz = fields.at[5], fields.at[6], fields.at[7]
    rho = fields.at[8]

    def wave(i, carry):
        for yc in range(nyc):
            pk = packed[yc, i]
            for f in range(NWIDE, NWIDE + NTHIN):
                fields[f, yc, 1, i] = pltpu.roll(pk, LANES - centre(f), 1)
        y0, z0 = get(by, i), get(bz, i)
        cx = (get(bx, i) + get(bx, i + 1)) * 0.5
        cy = (y0 + y0.y(1)) * 0.5
        cz = (z0 + z0.z(1)) * 0.5
        a, b, c = get(vx, i), get(vy, i), get(vz, i)
        square = cx * cx + cy * cy + cz * cz
        put(
            speed, i,
            sqrt(a * a + b * b + c * c) + sqrt(get(t0, i) * GAMMA + square / get(rho, i)),
        )
        return carry

    lax.fori_loop(nx - 2, 2 * nx + 2, wave, 0)

    def corner_means(i, carry):
        s0, sm = get(speed, i), get(speed, i - 1)
        a, b, c = get(vx, i), get(vy, i), get(vz, i)
        am, bm, cm = get(vx, i - 1), get(vy, i - 1), get(vz, i - 1)

        def store(k, sheet, scale):
            put(means.at[k], i, sheet * scale)

        def along(s, direction):
            return s + (s.y(-1) if direction == 1 else s.z(-1))

        store(0, along(along(c, 1), 2), 0.125)
        store(1, along(along(b, 1), 2), 0.125)
        store(2, along(along(s0, 1), 2), 0.125)
        store(3, along(a + am, 2), 0.125)
        store(4, along(c + cm, 2), 0.125)
        store(5, along(s0 + sm, 2), 0.125)
        store(6, along(b + bm, 1), 0.125)
        store(7, along(a + am, 1), 0.125)
        store(8, along(s0 + sm, 1), 0.125)
        return carry

    lax.fori_loop(nx - 1, 2 * nx + 2, corner_means, 0)

    def edge_fields(fx, fy, fz, i):
        x0, y0, z0 = get(fx, i), get(fy, i), get(fz, i)
        ym, zm = get(fy, i - 1), get(fz, i - 1)

        def edge(k, a0, a1, b0, b1):
            mb, ma, ms = [get(means.at[3 * k + n], i) for n in range(3)]
            put(
                edges.at[k], i,
                mb * (a0 + a1) - ma * (b0 + b1) + ms * (b0 - b1) - ms * (a0 - a1),
            )

        edge(0, y0, y0.z(-1), z0, z0.y(-1))
        edge(1, z0, zm, x0, x0.z(-1))
        edge(2, x0, x0.y(-1), y0, ym)

    def curl(i):
        ex, ey, ez = [get(edges.at[n], i) for n in range(3)]
        eyp, ezp = get(edges.at[1], i + 1), get(edges.at[2], i + 1)
        return (
            (ez.y(1) - ez) - (ey.z(1) - ey),
            (ex.z(1) - ex) - (ezp - ez),
            (eyp - ey) - (ex.y(1) - ex),
        )

    def first_edges(i, carry):
        edge_fields(bx, by, bz, i)
        return carry

    lax.fori_loop(nx - 1, 2 * nx + 2, first_edges, 0)

    def to_mid(i, carry):
        for n, part in enumerate(curl(i)):
            put(mid.at[n], i, get(fields.at[2 + n], i) - part * dt)
        return carry

    lax.fori_loop(nx - 1, 2 * nx + 1, to_mid, 0)

    def second_edges(i, carry):
        edge_fields(mid.at[0], mid.at[1], mid.at[2], i)
        return carry

    lax.fori_loop(nx, 2 * nx + 1, second_edges, 0)

    def to_end(i, carry):
        for n, part in enumerate(curl(i)):
            end = get(mid.at[n], i) - part * dt
            value = (get(fields.at[2 + n], i) + end) * 0.5
            b_out[n, i - nx] = value.parts[0][0]
        return carry

    lax.fori_loop(nx, 2 * nx, to_end, 0)

    for c in sends:
        c.wait_send()


def solution(mesh):
    sizes = tuple(mesh.shape[a] for a in AXES)
    nyc = 2 if sizes[1] == 2 else 3

    def on_device(t, d, b, v, r):
        nx = t.shape[0]
        planes = 3 * nx
        tile = (ROWS, LANES)
        ring = (nyc, 2, planes) + tile
        vm = lambda *shape: pltpu.VMEM(shape, jnp.float32)
        rounds = sum(sizes) - 3
        return pl.pallas_call(
            functools.partial(kernel, sizes, nx),
            out_shape=(
                jax.ShapeDtypeStruct(t.shape, jnp.float32),
                jax.ShapeDtypeStruct(b.shape, jnp.float32),
            ),
            in_specs=[pl.BlockSpec(memory_space=pl.ANY)] * 5,
            out_specs=[pl.BlockSpec(memory_space=pltpu.VMEM)] * 2,
            scratch_shapes=[
                vm(NWIDE + NTHIN, *ring),
                vm(nyc, planes, *tile),
                vm(nx, *tile),
                vm(2, nx, *tile),
                vm(3, *tile),
                vm(sizes[0] - 1, *tile),
                vm(sizes[1] - 1, *tile),
                vm(sizes[2] - 1, *tile),
                vm(*ring),
                vm(9, *ring),
                vm(*ring),
                vm(*ring),
                vm(*ring),
                vm(*ring),
                vm(9, *ring),
                vm(3, *ring),
                vm(3, *ring),
                pltpu.SemaphoreType.DMA((5,)),
                pltpu.SemaphoreType.DMA((rounds,)),
                pltpu.SemaphoreType.DMA((rounds,)),
                pltpu.SemaphoreType.DMA((2,)),
                pltpu.SemaphoreType.DMA((2,)),
                pltpu.SemaphoreType.DMA((3, 2)),
                pltpu.SemaphoreType.DMA((3, 2)),
                pltpu.SemaphoreType.DMA((6, 2)),
                pltpu.SemaphoreType.DMA((6, 2)),
            ],
            compiler_params=pltpu.CompilerParams(
                collective_id=0, has_side_effects=True, vmem_limit_bytes=48 * 1024 * 1024
            ),
        )(t, d, b, v, r)

    return jax.shard_map(
        on_device,
        mesh=mesh,
        in_specs=(
            P("gx", "gy", "gz"),
            P("gx", "gy", "gz"),
            P(None, "gx", "gy", "gz"),
            P(None, "gx", "gy", "gz"),
            P("gx", "gy", "gz"),
        ),
        out_specs=(P("gx", "gy", "gz"), P(None, "gx", "gy", "gz")),
        check_vma=False,
    )
```

time: 199 us -> 54.3 us (0.27); the launches traced: 195 us -> 54 us
  Pallas kernels: 0 us -> 48 us
  other arithmetic: 47.3 us -> 0 us
  starting transfers between devices: 42.6 us -> 0 us
  blocking collectives: 38.8 us -> 0 us
  local copies, waits for them, and re-layouts: 34.2 us -> 5.31 us
  waiting for transfers between devices: 21.5 us -> 0 us
  between operations: 11 us -> 0.65 us
    pallas_call x0 -> x1, Pallas kernels: none -> 48 us  [on_device(): pl.pallas_call(functools.partial(kernel, sizes, nx), out_shape=(jax.Shape...]
    ppermute x30 -> x0, starting transfers between devices: 42.6 us -> none  [the longest x15 25.4 us: extended(): lax.ppermute(lax.slice_in_dim(block, block.shape[dim] - width, None, axis...]
    pmin x1 -> x0, blocking collectives: 38.8 us -> none  [on_device(): interval_increment = lax.pmin(local_step, ('gx', 'gy', 'gz'))]
    ppermute x30 -> x0, waiting for transfers between devices: 21.5 us -> none  [the longest x15 11.5 us: extended(): lax.ppermute(lax.slice_in_dim(block, block.shape[dim] - width, None, axis...]
    concatenate x13 -> x0, other arithmetic: 13.2 us -> none  [extended(): block = jnp.concatenate([low, block, high], axis=dim)]
    concatenate x4 -> x0, local copies, waits for them, and re-layouts: 12.8 us -> none  [the longest x3 12 us: extended(): block = jnp.concatenate([low, block, high], axis=dim)]
    ppermute x4 -> x0, local copies, waits for them, and re-layouts: 12.7 us -> none  [the longest x2 6.36 us: extended(): lax.ppermute(lax.slice_in_dim(block, 0, width, axis=dim), axis, backward)]
    neg x24 -> x0, other arithmetic: 10.4 us -> none  [diffuse_thermal(): -(along_normal * (shifted(REFERENCE_SPOT) - shifted(backward)) + along_fi...]
  transfers between devices with their start and end apart: 30 -> 0, of which waited for: 18 -> 0; matrix products, arithmetic and copies ran while one was open for 14% -> 0% of each run, Pallas kernels for 0% -> 0%
where the time goes in v1:
time: 54.3 us; the launch traced here: 54 us
  Pallas kernels  48 us (88%)
  local copies, waits for them, and re-layouts  5.31 us (10%)
  between operations  0.65 us (1%)
    pallas_call x1, Pallas kernels, on_device(): pl.pallas_call(functools.partial(kernel, sizes, nx), out_shape=(jax.Shape...  48 us
    unnamed x12, local copies, waits for them, and re-layouts  5.31 us

profile of v1, /device:TPU:1, one launch (start us, length us, event | category | flops | bytes accessed | tf_op | source)
XLA Modules:
  0.0 54.0 jit_solution(922424997849803337)
XLA Ops:
  0.6 0.0 copy-start
  0.6 0.9 %copy-done = f32[3,8,8,128]{3,2,1,0:T(8,128)S(1)} copy-done((f32[3,8,8,128]{3,2,1,0:T(8,128)S(1)}, f32[3,8,8,128]{3,2,1,0:T(8,128)}, u32[]{:S(2)}) %copy-start) | copy-done | bytes 98328
  1.5 0.0 copy-start.1
  1.5 0.9 %copy-done.1 = f32[3,8,8,128]{3,2,1,0:T(8,128)S(1)} copy-done((f32[3,8,8,128]{3,2,1,0:T(8,128)S(1)}, f32[3,8,8,128]{3,2,1,0:T(8,128)}, u32[]{:S(2)}) %copy-start.1) | copy-done | bytes 98328
  2.4 0.0 copy-start.2
  2.4 0.8 %copy-done.2 = f32[8,8,128]{2,1,0:T(8,128)S(1)} copy-done((f32[8,8,128]{2,1,0:T(8,128)S(1)}, f32[8,8,128]{2,1,0:T(8,128)}, u32[]{:S(2)}) %copy-start.2) | copy-done | bytes 32792
  3.2 0.0 copy-start.3
  3.2 0.8 %copy-done.3 = f32[8,8,128]{2,1,0:T(8,128)S(1)} copy-done((f32[8,8,128]{2,1,0:T(8,128)S(1)}, f32[8,8,128]{2,1,0:T(8,128)}, u32[]{:S(2)}) %copy-start.3) | copy-done | bytes 32792
  3.9 0.0 copy-start.4
  3.9 0.8 %copy-done.4 = f32[8,8,128]{2,1,0:T(8,128)S(1)} copy-done((f32[8,8,128]{2,1,0:T(8,128)S(1)}, f32[8,8,128]{2,1,0:T(8,128)}, u32[]{:S(2)}) %copy-start.4) | copy-done | bytes 32792
  4.7 48.0 %shard_map.68 = (f32[8,8,128]{2,1,0:T(8,128)S(1)}, f32[3,8,8,128]{3,2,1,0:T(8,128)S(1)}) custom-call(f32[8,8,128]{2,1,0:T(8,128)S(1)} %copy-done.2, f32[8,8,128]{2,1,0:T(8,128)S(1)} %copy-done.3, f32[3,8,8,128]{3,2,1,0:T(8,128)S(1)} %copy-done, f32[3,8,8,128]{3,2,1,0:T(8,128)S(1)} %copy-done.1, f32[8,8,128]{2,1,0:T(8,128)S(1)} %copy-done.4), custom_call_target="tpu_custom_call" | custom-call | tf_op jit(solution)/shard_map/pallas_call | solution.py:495
  52.7 0.6 %copy.9 = f32[8,8,128]{2,1,0:T(8,128)} copy(f32[8,8,128]{2,1,0:T(8,128)S(1)} %get-tuple-element.4) | data formatting | bytes 65536
  53.3 0.6 %copy.10 = f32[3,8,8,128]{3,2,1,0:T(8,128)} copy(f32[3,8,8,128]{3,2,1,0:T(8,128)S(1)} %get-tuple-element.5) | data formatting | bytes 196608
Async XLA Ops:
  0.6 0.9 %copy-start = (f32[3,8,8,128]{3,2,1,0:T(8,128)S(1)}, f32[3,8,8,128]{3,2,1,0:T(8,128)}, u32[]{:S(2)}) copy-start(f32[3,8,8,128]{3,2,1,0:T(8,128)} %b_in.1) | copy-start | bytes 294916
  1.5 0.9 %copy-start.1 = (f32[3,8,8,128]{3,2,1,0:T(8,128)S(1)}, f32[3,8,8,128]{3,2,1,0:T(8,128)}, u32[]{:S(2)}) copy-start(f32[3,8,8,128]{3,2,1,0:T(8,128)} %v_in.1) | copy-start | bytes 294916
  2.4 0.8 %copy-start.2 = (f32[8,8,128]{2,1,0:T(8,128)S(1)}, f32[8,8,128]{2,1,0:T(8,128)}, u32[]{:S(2)}) copy-start(f32[8,8,128]{2,1,0:T(8,128)} %t_in.1) | copy-start | bytes 98308
  3.2 0.8 %copy-start.3 = (f32[8,8,128]{2,1,0:T(8,128)S(1)}, f32[8,8,128]{2,1,0:T(8,128)}, u32[]{:S(2)}) copy-start(f32[8,8,128]{2,1,0:T(8,128)} %d_in.1) | copy-start | bytes 98308
  3.9 0.8 %copy-start.4 = (f32[8,8,128]{2,1,0:T(8,128)S(1)}, f32[8,8,128]{2,1,0:T(8,128)}, u32[]{:S(2)}) copy-start(f32[8,8,128]{2,1,0:T(8,128)} %r_in.1) | copy-start | bytes 98308

commit v2 on v1

--- a/solution.py
+++ b/solution.py
@@ -275,7 +275,7 @@
                 kappa[yc, zc, i] = fields[1, yc, zc, i] * (t * t * jnp.sqrt(t))
         return carry
 
-    lax.fori_loop(0, 3 * nx, unpack, 0)
+    lax.fori_loop(0, 3 * nx, unpack, 0, unroll=3)
 
     bx, by, bz = fields.at[2], fields.at[3], fields.at[4]
     t0 = fields.at[0]
@@ -303,7 +303,7 @@
         store(2, (k0 + k0.z(-1)) * 0.5, z0, (xx + xx.z(-1)) * 0.25, (yy + yy.z(-1)) * 0.25)
         return carry
 
-    lax.fori_loop(1, 3 * nx, coefficients, 0)
+    lax.fori_loop(1, 3 * nx, coefficients, 0, unroll=2)
 
     def conduct(u, reach, finish):
         def ahead(i, u0, u1, dy0, dz0):
@@ -341,7 +341,7 @@
             finish(i, u0, (gx1 - gx0) + (gy.y(1) - gy) + (gz.z(1) - gz))
             return flat(u0, u1, u1ym, u1zm, dy1, dz1, gx1)
 
-        lax.fori_loop(first, 2 * nx + reach, step, flat(um, u0, u0ym, u0zm, dy0, dz0, gx0))
+        lax.fori_loop(first, 2 * nx + reach, step, flat(um, u0, u0ym, u0zm, dy0, dz0, gx0), unroll=4)
 
     for c in red_x:
         c.wait_recv()
@@ -399,7 +399,7 @@
         )
         return carry
 
-    lax.fori_loop(nx - 2, 2 * nx + 2, wave, 0)
+    lax.fori_loop(nx - 2, 2 * nx + 2, wave, 0, unroll=4)
 
     def corner_means(i, carry):
         s0, sm = get(speed, i), get(speed, i - 1)
@@ -423,7 +423,7 @@
         store(8, along(s0 + sm, 1), 0.125)
         return carry
 
-    lax.fori_loop(nx - 1, 2 * nx + 2, corner_means, 0)
+    lax.fori_loop(nx - 1, 2 * nx + 2, corner_means, 0, unroll=4)
 
     def edge_fields(fx, fy, fz, i):
         x0, y0, z0 = get(fx, i), get(fy, i), get(fz, i)
@@ -453,20 +453,20 @@
         edge_fields(bx, by, bz, i)
         return carry
 
-    lax.fori_loop(nx - 1, 2 * nx + 2, first_edges, 0)
+    lax.fori_loop(nx - 1, 2 * nx + 2, first_edges, 0, unroll=4)
 
     def to_mid(i, carry):
         for n, part in enumerate(curl(i)):
             put(mid.at[n], i, get(fields.at[2 + n], i) - part * dt)
         return carry
 
-    lax.fori_loop(nx - 1, 2 * nx + 1, to_mid, 0)
+    lax.fori_loop(nx - 1, 2 * nx + 1, to_mid, 0, unroll=4)
 
     def second_edges(i, carry):
         edge_fields(mid.at[0], mid.at[1], mid.at[2], i)
         return carry
 
-    lax.fori_loop(nx, 2 * nx + 1, second_edges, 0)
+    lax.fori_loop(nx, 2 * nx + 1, second_edges, 0, unroll=4)
 
     def to_end(i, carry):
         for n, part in enumerate(curl(i)):
@@ -475,7 +475,7 @@
             b_out[n, i - nx] = value.parts[0][0]
         return carry
 
-    lax.fori_loop(nx, 2 * nx, to_end, 0)
+    lax.fori_loop(nx, 2 * nx, to_end, 0, unroll=4)
 
     for c in sends:
         c.wait_send()
@@ -498,7 +498,7 @@
                 jax.ShapeDtypeStruct(t.shape, jnp.float32),
                 jax.ShapeDtypeStruct(b.shape, jnp.float32),
             ),
-            in_specs=[pl.BlockSpec(memory_space=pl.ANY)] * 5,
+            in_specs=[pl.BlockSpec(memory_space=pltpu.HBM)] * 5,
             out_specs=[pl.BlockSpec(memory_space=pltpu.VMEM)] * 2,
             scratch_shapes=[
                 vm(NWIDE + NTHIN, *ring),
@@ -529,7 +529,7 @@
                 pltpu.SemaphoreType.DMA((6, 2)),
             ],
             compiler_params=pltpu.CompilerParams(
-                collective_id=0, has_side_effects=True, vmem_limit_bytes=48 * 1024 * 1024
+                collective_id=0, has_side_effects=True, vmem_limit_bytes=67043328
             ),
         )(t, d, b, v, r)
 

time: 54.3 us -> 36.1 us (0.66)
  Pallas kernels: 48 us -> 32.3 us
  local copies, waits for them, and re-layouts: 5.31 us -> 2.91 us
    pallas_call x1, Pallas kernels: 48 us -> 32.3 us  [on_device(): pl.pallas_call(functools.partial(kernel, sizes, nx), out_shape=(jax.Shape...]
    unnamed x12 -> x2, local copies, waits for them, and re-layouts: 5.31 us -> 2.91 us
where the time goes in v2:
time: 36.1 us; the launch traced here: 35.9 us
  Pallas kernels  32.3 us (89%)
  local copies, waits for them, and re-layouts  2.91 us (8%)
  between operations  0.64 us (2%)
    pallas_call x1, Pallas kernels, on_device(): pl.pallas_call(functools.partial(kernel, sizes, nx), out_shape=(jax.Shape...  32.3 us
    unnamed x2, local copies, waits for them, and re-layouts  2.91 us

profile of v2, /device:TPU:1, one launch (start us, length us, event | category | flops | bytes accessed | tf_op | source)
XLA Modules:
  0.0 35.9 jit_solution(6485134980709091271)
XLA Ops:
  0.6 32.3 %shard_map.68 = (f32[8,8,128]{2,1,0:T(8,128)}, f32[3,8,8,128]{3,2,1,0:T(8,128)}) custom-call(f32[8,8,128]{2,1,0:T(8,128)} %t_in.1, f32[8,8,128]{2,1,0:T(8,128)} %d_in.1, f32[3,8,8,128]{3,2,1,0:T(8,128)} %b_in.1, f32[3,8,8,128]{3,2,1,0:T(8,128)} %v_in.1, f32[8,8,128]{2,1,0:T(8,128)} %r_in.1), custom_call_target="tpu_custom_call" | custom-call | tf_op jit(solution)/shard_map/pallas_call | solution.py:495
  33.0 1.4 %copy.9 = f32[8,8,128]{2,1,0:T(8,128)} copy(f32[8,8,128]{2,1,0:T(8,128)} %get-tuple-element.4) | data formatting | bytes 65536
  34.4 1.5 %copy.10 = f32[3,8,8,128]{3,2,1,0:T(8,128)} copy(f32[3,8,8,128]{3,2,1,0:T(8,128)} %get-tuple-element.5) | data formatting | bytes 196608

commit v3 on v2

--- a/solution.py
+++ b/solution.py
@@ -17,6 +17,7 @@
 LANES = 128
 WIDE = SECTIONS
 THIN = 4
+NEAR = 2
 NWIDE = 5
 NTHIN = 4
 
@@ -227,7 +228,10 @@
             remote(mine, ends.at[1], z_send.at[1], z_recv.at[1], at("gz", -1)),
         ]
     )
-    y_wide = go(y_copies(0, lambda c: fields.at[wide, c, 0, own]))
+    pieces = (pl.ds(0, 2), pl.ds(2, 3))
+    y_wide = [
+        go(y_copies(n, lambda c, f=f: fields.at[f, c, 0, own])) for n, f in enumerate(pieces)
+    ]
     x_wide = go(x_copies(0, lambda r: fields.at[wide, 0, 0, r], nx))
 
     for c in red_y:
@@ -235,35 +239,32 @@
     for k in range(counts["gy"] - 1):
         top = jnp.maximum(top, parts_y[k])
     kmax[1] = top
+    red_z = go(reduce_round("gz", kmax.at[1], parts_z))
     for c in z_ends:
         c.wait_recv()
     in_wide = lane < 2 * WIDE * NWIDE
     upper = jnp.where(in_wide, lane % (2 * WIDE) - WIDE, lane % (2 * THIN) - THIN) >= 0
     for i in range(nx):
         packed[0, nx + i] = jnp.where(upper, ends[1, i], ends[0, i])
-    red_z = go(reduce_round("gz", kmax.at[1], parts_z))
-    y_pack = go(y_copies(1, lambda c: packed.at[c, own]))
-    y_thin = go(y_copies(2, lambda c: fields.at[thin, c, 0, own]))
-    x_pack = go(x_copies(1, lambda r: packed.at[0, r], nx))
-
     for c in red_z:
         c.wait_recv()
     for k in range(counts["gz"] - 1):
         top = jnp.maximum(top, parts_z[k])
     kmax[2] = top
-    for c in y_wide:
-        c.wait_recv()
+    y_pack = go(y_copies(2, lambda c: packed.at[c, own]))
+    y_thin = go(y_copies(3, lambda c: fields.at[thin, c, 0, own]))
+    x_pack = go(x_copies(1, lambda r: packed.at[0, r], nx))
     red_x = go(reduce_round("gx", kmax.at[2], parts_x))
-    x_wide2 = go(x_copies(2, lambda r: fields.at[wide, rest, 0, r], nx))
+
+    x_wide2 = []
+    for n, f in enumerate(pieces):
+        for c in y_wide[n]:
+            c.wait_recv()
+        x_wide2 += go(x_copies(2 + n, lambda r, f=f: fields.at[f, rest, 0, r], nx))
     for c in y_pack:
         c.wait_recv()
-    x_pack2 = go(x_copies(3, lambda r: packed.at[rest, r], nx))
-    x_thin = go(x_copies(4, lambda r: fields.at[thin, 0, 0, r], THIN))
-    for c in y_thin:
-        c.wait_recv()
-    x_thin2 = go(x_copies(5, lambda r: fields.at[thin, rest, 0, r], THIN))
-    for c in x_wide + x_pack + x_wide2 + x_pack2:
-        c.wait_recv()
+    x_pack2 = go(x_copies(4, lambda r: packed.at[rest, r], nx))
+    x_thin = go(x_copies(5, lambda r: fields.at[thin, 0, 0, r], NEAR))
 
     def unpack(i, carry):
         for yc in range(nyc):
@@ -275,7 +276,7 @@
                 kappa[yc, zc, i] = fields[1, yc, zc, i] * (t * t * jnp.sqrt(t))
         return carry
 
-    lax.fori_loop(0, 3 * nx, unpack, 0, unroll=3)
+    lax.fori_loop(nx, 2 * nx, unpack, 0, unroll=4)
 
     bx, by, bz = fields.at[2], fields.at[3], fields.at[4]
     t0 = fields.at[0]
@@ -303,82 +304,7 @@
         store(2, (k0 + k0.z(-1)) * 0.5, z0, (xx + xx.z(-1)) * 0.25, (yy + yy.z(-1)) * 0.25)
         return carry
 
-    lax.fori_loop(1, 3 * nx, coefficients, 0, unroll=2)
-
-    def conduct(u, reach, finish):
-        def ahead(i, u0, u1, dy0, dz0):
-            u1ym, u1zm = u1.y(-1), u1.z(-1)
-            dy1, dz1 = u1.y(1) - u1ym, u1.z(1) - u1zm
-            if u0 is None:
-                return u1ym, u1zm, dy1, dz1, None
-            gx = (
-                get(coef.at[0], i) * (u1 - u0)
-                + get(coef.at[1], i) * (dy1 + dy0)
-                + get(coef.at[2], i) * (dz1 + dz0)
-            )
-            return u1ym, u1zm, dy1, dz1, gx
-
-        first = nx - reach
-        um, u0 = get(u, first - 1), get(u, first)
-        _, _, dym, dzm, _ = ahead(first - 1, None, um, None, None)
-        u0ym, u0zm, dy0, dz0, gx0 = ahead(first, um, u0, dym, dzm)
-
-        def step(i, carry):
-            um, u0, u0ym, u0zm, dy0, dz0, gx0 = unflat(carry, nyc)
-            u1 = get(u, i + 1)
-            u1ym, u1zm, dy1, dz1, gx1 = ahead(i + 1, u0, u1, dy0, dz0)
-            dx = u1 - um
-            gy = (
-                get(coef.at[3], i) * (u0 - u0ym)
-                + get(coef.at[4], i) * (dz0 + dz0.y(-1))
-                + get(coef.at[5], i) * (dx + dx.y(-1))
-            )
-            gz = (
-                get(coef.at[6], i) * (u0 - u0zm)
-                + get(coef.at[7], i) * (dx + dx.z(-1))
-                + get(coef.at[8], i) * (dy0 + dy0.z(-1))
-            )
-            finish(i, u0, (gx1 - gx0) + (gy.y(1) - gy) + (gz.z(1) - gz))
-            return flat(u0, u1, u1ym, u1zm, dy1, dz1, gx1)
-
-        lax.fori_loop(first, 2 * nx + reach, step, flat(um, u0, u0ym, u0zm, dy0, dz0, gx0), unroll=4)
-
-    for c in red_x:
-        c.wait_recv()
-    for k in range(counts["gx"] - 1):
-        top = jnp.maximum(top, parts_x[k])
-    limit = (SECTIONS * SECTIONS + SECTIONS - 2) / 16.0
-    peak = jnp.max(jnp.max(top, axis=0, keepdims=True), axis=1, keepdims=True)
-    dt = jnp.broadcast_to(limit / peak, (ROWS, LANES))
-
-    recipe = section_weights(SECTIONS)
-
-    def begin(i, u0, rate):
-        rate = rate * dt
-        put(rate0, i, rate)
-        put(ya, i, u0 + rate * recipe[1])
-
-    conduct(t0, SECTIONS - 1, begin)
-    newest, older = ya, yb
-    for j in range(2, SECTIONS + 1):
-        p, r, q, m, h = recipe[j]
-        m_dt = dt * m
-        prev2 = t0 if j == 2 else older
-
-        def advance(i, u0, rate):
-            value = (
-                u0 * p + get(prev2, i) * r + get(t0, i) * q + rate * m_dt + get(rate0, i) * h
-            )
-            if j == SECTIONS:
-                t_out[i - nx] = value.parts[0][0]
-            else:
-                put(older, i, value)
-
-        conduct(newest, SECTIONS - j, advance)
-        newest, older = older, newest
-
-    for c in x_thin + x_thin2:
-        c.wait_recv()
+    lax.fori_loop(nx + 1, 2 * nx - 1, coefficients, 0, unroll=2)
     vx, vy, vz = fields.at[5], fields.at[6], fields.at[7]
     rho = fields.at[8]
 
@@ -399,7 +325,6 @@
         )
         return carry
 
-    lax.fori_loop(nx - 2, 2 * nx + 2, wave, 0, unroll=4)
 
     def corner_means(i, carry):
         s0, sm = get(speed, i), get(speed, i - 1)
@@ -423,7 +348,6 @@
         store(8, along(s0 + sm, 1), 0.125)
         return carry
 
-    lax.fori_loop(nx - 1, 2 * nx + 2, corner_means, 0, unroll=4)
 
     def edge_fields(fx, fy, fz, i):
         x0, y0, z0 = get(fx, i), get(fy, i), get(fz, i)
@@ -440,6 +364,99 @@
         edge(1, z0, zm, x0, x0.z(-1))
         edge(2, x0, x0.y(-1), y0, ym)
 
+    def first_edges(i, carry):
+        edge_fields(bx, by, bz, i)
+        return carry
+
+    for c in y_thin:
+        c.wait_recv()
+    x_thin2 = go(x_copies(6, lambda r: fields.at[thin, rest, 0, r], NEAR))
+    lax.fori_loop(nx, 2 * nx - 1, wave, 0, unroll=2)
+    lax.fori_loop(nx + 1, 2 * nx - 1, corner_means, 0, unroll=3)
+    lax.fori_loop(nx + 1, 2 * nx - 1, first_edges, 0, unroll=3)
+
+    for c in x_wide + x_pack + x_wide2 + x_pack2:
+        c.wait_recv()
+    lax.fori_loop(0, nx, unpack, 0, unroll=4)
+    lax.fori_loop(2 * nx, 3 * nx, unpack, 0, unroll=4)
+    lax.fori_loop(1, nx + 1, coefficients, 0, unroll=2)
+    lax.fori_loop(2 * nx - 1, 3 * nx, coefficients, 0, unroll=3)
+
+
+    def conduct(u, reach, finish):
+        def ahead(i, u0, u1, dy0, dz0):
+            u1ym, u1zm = u1.y(-1), u1.z(-1)
+            dy1, dz1 = u1.y(1) - u1ym, u1.z(1) - u1zm
+            if u0 is None:
+                return u1ym, u1zm, dy1, dz1, None
+            gx = (
+                get(coef.at[0], i) * (u1 - u0)
+                + get(coef.at[1], i) * (dy1 + dy0)
+                + get(coef.at[2], i) * (dz1 + dz0)
+            )
+            return u1ym, u1zm, dy1, dz1, gx
+
+        first = nx - reach
+        um, u0 = get(u, first - 1), get(u, first)
+        _, _, dym, dzm, _ = ahead(first - 1, None, um, None, None)
+        u0ym, u0zm, dy0, dz0, gx0 = ahead(first, um, u0, dym, dzm)
+
+        def step(i, carry):
+            um, u0, u0ym, u0zm, dy0, dz0, gx0 = unflat(carry, nyc)
+            u1 = get(u, i + 1)
+            u1ym, u1zm, dy1, dz1, gx1 = ahead(i + 1, u0, u1, dy0, dz0)
+            dx = u1 - um
+            gy = (
+                get(coef.at[3], i) * (u0 - u0ym)
+                + get(coef.at[4], i) * (dz0 + dz0.y(-1))
+                + get(coef.at[5], i) * (dx + dx.y(-1))
+            )
+            gz = (
+                get(coef.at[6], i) * (u0 - u0zm)
+                + get(coef.at[7], i) * (dx + dx.z(-1))
+                + get(coef.at[8], i) * (dy0 + dy0.z(-1))
+            )
+            finish(i, u0, (gx1 - gx0) + (gy.y(1) - gy) + (gz.z(1) - gz))
+            return flat(u0, u1, u1ym, u1zm, dy1, dz1, gx1)
+
+        lax.fori_loop(first, 2 * nx + reach, step, flat(um, u0, u0ym, u0zm, dy0, dz0, gx0), unroll=4)
+
+    for c in red_x:
+        c.wait_recv()
+    for k in range(counts["gx"] - 1):
+        top = jnp.maximum(top, parts_x[k])
+    limit = (SECTIONS * SECTIONS + SECTIONS - 2) / 16.0
+    peak = jnp.max(jnp.max(top, axis=0, keepdims=True), axis=1, keepdims=True)
+    dt = jnp.broadcast_to(limit / peak, (ROWS, LANES))
+
+    recipe = section_weights(SECTIONS)
+
+    def begin(i, u0, rate):
+        rate = rate * dt
+        put(rate0, i, rate)
+        put(ya, i, u0 + rate * recipe[1])
+
+    conduct(t0, SECTIONS - 1, begin)
+    newest, older = ya, yb
+    for j in range(2, SECTIONS + 1):
+        p, r, q, m, h = recipe[j]
+        m_dt = dt * m
+        prev2 = t0 if j == 2 else older
+
+        def advance(i, u0, rate):
+            value = (
+                u0 * p + get(prev2, i) * r + get(t0, i) * q + rate * m_dt + get(rate0, i) * h
+            )
+            if j == SECTIONS:
+                t_out[i - nx] = value.parts[0][0]
+            else:
+                put(older, i, value)
+
+        conduct(newest, SECTIONS - j, advance)
+        newest, older = older, newest
+
+    for c in x_thin + x_thin2:
+        c.wait_recv()
     def curl(i):
         ex, ey, ez = [get(edges.at[n], i) for n in range(3)]
         eyp, ezp = get(edges.at[1], i + 1), get(edges.at[2], i + 1)
@@ -449,11 +466,11 @@
             (eyp - ey) - (ex.y(1) - ex),
         )
 
-    def first_edges(i, carry):
-        edge_fields(bx, by, bz, i)
-        return carry
-
-    lax.fori_loop(nx - 1, 2 * nx + 2, first_edges, 0, unroll=4)
+    for lo, hi in ((nx - 2, nx), (2 * nx - 1, 2 * nx + 2)):
+        lax.fori_loop(lo, hi, wave, 0, unroll=hi - lo)
+    for lo, hi in ((nx - 1, nx + 1), (2 * nx - 1, 2 * nx + 2)):
+        lax.fori_loop(lo, hi, corner_means, 0, unroll=hi - lo)
+        lax.fori_loop(lo, hi, first_edges, 0, unroll=hi - lo)
 
     def to_mid(i, carry):
         for n, part in enumerate(curl(i)):
@@ -523,10 +540,10 @@
                 pltpu.SemaphoreType.DMA((rounds,)),
                 pltpu.SemaphoreType.DMA((2,)),
                 pltpu.SemaphoreType.DMA((2,)),
-                pltpu.SemaphoreType.DMA((3, 2)),
-                pltpu.SemaphoreType.DMA((3, 2)),
-                pltpu.SemaphoreType.DMA((6, 2)),
-                pltpu.SemaphoreType.DMA((6, 2)),
+                pltpu.SemaphoreType.DMA((4, 2)),
+                pltpu.SemaphoreType.DMA((4, 2)),
+                pltpu.SemaphoreType.DMA((7, 2)),
+                pltpu.SemaphoreType.DMA((7, 2)),
             ],
             compiler_params=pltpu.CompilerParams(
                 collective_id=0, has_side_effects=True, vmem_limit_bytes=67043328

time: 36.1 us -> 32.7 us (0.906)
  Pallas kernels: 32.3 us -> 28.9 us
    pallas_call x1, Pallas kernels: 32.3 us -> 28.9 us  [on_device(): pl.pallas_call(functools.partial(kernel, sizes, nx), out_shape=(jax.Shape...]
where the time goes in v3:
time: 32.7 us; the launch traced here: 32.4 us
  Pallas kernels  28.9 us (88%)
  local copies, waits for them, and re-layouts  2.91 us (9%)
  between operations  0.64 us (2%)
    pallas_call x1, Pallas kernels, on_device(): pl.pallas_call(functools.partial(kernel, sizes, nx), out_shape=(jax.Shape...  28.9 us
    unnamed x2, local copies, waits for them, and re-layouts  2.91 us

profile of v3, /device:TPU:1, one launch (start us, length us, event | category | flops | bytes accessed | tf_op | source)
XLA Modules:
  0.0 32.4 jit_solution(12277994008971131500)
XLA Ops:
  0.6 28.9 %shard_map.68 = (f32[8,8,128]{2,1,0:T(8,128)}, f32[3,8,8,128]{3,2,1,0:T(8,128)}) custom-call(f32[8,8,128]{2,1,0:T(8,128)} %t_in.1, f32[8,8,128]{2,1,0:T(8,128)} %d_in.1, f32[3,8,8,128]{3,2,1,0:T(8,128)} %b_in.1, f32[3,8,8,128]{3,2,1,0:T(8,128)} %v_in.1, f32[8,8,128]{2,1,0:T(8,128)} %r_in.1), custom_call_target="tpu_custom_call" | custom-call | tf_op jit(solution)/shard_map/pallas_call | solution.py:512
  29.5 1.4 %copy.9 = f32[8,8,128]{2,1,0:T(8,128)} copy(f32[8,8,128]{2,1,0:T(8,128)} %get-tuple-element.4) | data formatting | bytes 65536
  30.9 1.5 %copy.10 = f32[3,8,8,128]{3,2,1,0:T(8,128)} copy(f32[3,8,8,128]{3,2,1,0:T(8,128)} %get-tuple-element.5) | data formatting | bytes 196608

commit v4 on v3

--- a/solution.py
+++ b/solution.py
@@ -419,7 +419,7 @@
             finish(i, u0, (gx1 - gx0) + (gy.y(1) - gy) + (gz.z(1) - gz))
             return flat(u0, u1, u1ym, u1zm, dy1, dz1, gx1)
 
-        lax.fori_loop(first, 2 * nx + reach, step, flat(um, u0, u0ym, u0zm, dy0, dz0, gx0), unroll=4)
+        lax.fori_loop(first, 2 * nx + reach, step, flat(um, u0, u0ym, u0zm, dy0, dz0, gx0), unroll=(nx + 2 * reach) // 2)
 
     for c in red_x:
         c.wait_recv()

time: 32.7 us -> 32 us (0.979)
  Pallas kernels: 28.9 us -> 28.2 us
    pallas_call x1, Pallas kernels: 28.9 us -> 28.2 us  [on_device(): pl.pallas_call(functools.partial(kernel, sizes, nx), out_shape=(jax.Shape...]
where the time goes in v4:
time: 32 us; the launch traced here: 31.8 us
  Pallas kernels  28.2 us (88%)
  local copies, waits for them, and re-layouts  2.91 us (9%)
  between operations  0.64 us (2%)
    pallas_call x1, Pallas kernels, on_device(): pl.pallas_call(functools.partial(kernel, sizes, nx), out_shape=(jax.Shape...  28.2 us
    unnamed x2, local copies, waits for them, and re-layouts  2.91 us

profile of v4, /device:TPU:1, one launch (start us, length us, event | category | flops | bytes accessed | tf_op | source)
XLA Modules:
  0.0 31.8 jit_solution(3164671317728406616)
XLA Ops:
  0.6 28.2 %shard_map.68 = (f32[8,8,128]{2,1,0:T(8,128)}, f32[3,8,8,128]{3,2,1,0:T(8,128)}) custom-call(f32[8,8,128]{2,1,0:T(8,128)} %t_in.1, f32[8,8,128]{2,1,0:T(8,128)} %d_in.1, f32[3,8,8,128]{3,2,1,0:T(8,128)} %b_in.1, f32[3,8,8,128]{3,2,1,0:T(8,128)} %v_in.1, f32[8,8,128]{2,1,0:T(8,128)} %r_in.1), custom_call_target="tpu_custom_call" | custom-call | tf_op jit(solution)/shard_map/pallas_call | solution.py:512
  28.9 1.4 %copy.9 = f32[8,8,128]{2,1,0:T(8,128)} copy(f32[8,8,128]{2,1,0:T(8,128)} %get-tuple-element.4) | data formatting | bytes 65536
  30.2 1.5 %copy.10 = f32[3,8,8,128]{3,2,1,0:T(8,128)} copy(f32[3,8,8,128]{3,2,1,0:T(8,128)} %get-tuple-element.5) | data formatting | bytes 196608
